TPU v7x, 8 devices: a whole 2x2x1 slice. The times are simulated.
8 devices in a mesh: dp: 1 (over z), tp: 2 (over y), ep: 4 (over x, core).
Axes of the slice: x: 2, y: 2, z: 1, core: 2. Of those that a mesh axis runs over, the one named last changes fastest.
Arguments:
- hidden_in: bfloat16 [32, 256, 1024], P(('dp', 'ep'), 'tp')
- ln_attn: float32 [2, 1024], replicated
- ln_ffn: float32 [2, 1024], replicated
- w_query: bfloat16 [2, 1024, 1024], P(None, None, 'tp')
- w_key: bfloat16 [2, 1024, 1024], P(None, None, 'tp')
- w_value: bfloat16 [2, 1024, 1024], P(None, None, 'tp')
- w_out: bfloat16 [2, 1024, 1024], P(None, 'tp')
- bias_table: float32 [2, 16, 32], P(None, 'tp')
- w_gate: bfloat16 [1024, 512], P(None, 'tp')
- w_up: bfloat16 [1024, 512], P(None, 'tp')
- w_down: bfloat16 [512, 1024], P('tp')
- w_router: float32 [1024, 32], replicated
- expert_in: bfloat16 [32, 1024, 512], P(('tp', 'ep'))
- expert_out: bfloat16 [32, 512, 1024], P(('tp', 'ep'))
- expert_ids: int32 [32, 256, 2], P(('dp', 'ep'), 'tp')
Outputs:
- output 1: bfloat16 [32, 256, 1024], P(('dp', 'ep'), 'tp')
- output 2: bfloat16 [2, 32, 16, 256, 64], P(None, ('dp', 'ep'), 'tp')
- output 3: bfloat16 [2, 32, 16, 256, 64], P(None, ('dp', 'ep'), 'tp')
All inputs are finite; a program needn't handle non-finite values.
Results may differ from a plain program's by a relative error of at most 0.0146873.
Values are sent between devices in bfloat16 or wider.
A program may use at most 1 GiB of HBM per device.

v0:
```python
import jax
import jax.numpy as jnp
from jax import lax
from jax.sharding import PartitionSpec as P

EXACT_BUCKETS = 16
THRESHOLDS = (18, 20, 23, 26, 30, 34, 39, 45, 51, 58, 66, 76, 86, 98, 112)
EPSILON = 1e-6


def bucket_of(rel_pos):
    bucket_idx = jnp.minimum(rel_pos, EXACT_BUCKETS)
    for threshold in THRESHOLDS:
        bucket_idx = bucket_idx + (rel_pos >= threshold).astype(jnp.int32)
    return bucket_idx


def rms_norm(rows_in, ln_scale):
    wide_rows = rows_in.astype(jnp.float32)
    inv_rms = lax.rsqrt(jnp.mean(wide_rows * wide_rows, axis=-1, keepdims=True) + EPSILON)
    return (wide_rows * inv_rms * ln_scale).astype(jnp.bfloat16)


def causal_bias(bias_rows, seq_len):
    positions = jnp.arange(seq_len)
    rel_pos = positions[:, None] - positions[None, :]
    bias_full = jnp.take(bias_rows, bucket_of(jnp.maximum(rel_pos, 0)), axis=1)
    return jnp.where(rel_pos[None] >= 0, bias_full, -jnp.inf)


def attend(normed_full, w_query, w_key, w_value, bias_rows):
    local_batch, seq_len, d_model = normed_full.shape
    num_heads = bias_rows.shape[0]
    head_dim = w_query.shape[1] // num_heads

    def project(weight):
        projected = jnp.einsum('btd,dk->btk', normed_full, weight, preferred_element_type=jnp.float32)
        return projected.astype(jnp.bfloat16).reshape(local_batch, seq_len, num_heads, head_dim)

    queries = project(w_query)
    keys_full = project(w_key)
    values_full = project(w_value)
    scores = jnp.einsum('bqhd,bkhd->bhqk', queries, keys_full, preferred_element_type=jnp.float32)
    scores = scores * (head_dim ** -0.5) + causal_bias(bias_rows, seq_len)[None]
    attn_probs = jax.nn.softmax(scores, axis=-1).astype(jnp.bfloat16)
    context = jnp.einsum('bhqk,bkhd->bqhd', attn_probs, values_full, preferred_element_type=jnp.float32)
    context = context.astype(jnp.bfloat16).reshape(local_batch, seq_len, num_heads * head_dim)
    return context, jnp.swapaxes(keys_full, 1, 2), jnp.swapaxes(values_full, 1, 2)


def attention_block(hidden, ln_scale, w_query, w_key, w_value, w_out, bias_rows):
    normed = rms_norm(hidden, ln_scale)
    gathered = lax.all_gather(normed, 'tp', axis=1, tiled=True)
    context, keys_cache, values_cache = attend(gathered, w_query, w_key, w_value, bias_rows)
    part_sum = jnp.einsum('crl,le->cre', context, w_out, preferred_element_type=jnp.float32)
    reduced = lax.psum_scatter(part_sum, 'tp', scatter_dimension=1, tiled=True)
    return (hidden.astype(jnp.float32) + reduced).astype(jnp.bfloat16), keys_cache, values_cache


def ffn_block(hidden, ln_scale, w_gate, w_up, w_down):
    normed = rms_norm(hidden, ln_scale)
    gathered = lax.all_gather(normed, 'tp', axis=1, tiled=True)
    gate_pre = jnp.einsum('btd,df->btf', gathered, w_gate, preferred_element_type=jnp.float32)
    up_pre = jnp.einsum('btd,df->btf', gathered, w_up, preferred_element_type=jnp.float32)
    ffn_hidden = (jax.nn.gelu(gate_pre) * up_pre).astype(jnp.bfloat16)
    part_sum = jnp.einsum('btf,fd->btd', ffn_hidden, w_down, preferred_element_type=jnp.float32)
    reduced = lax.psum_scatter(part_sum, 'tp', scatter_dimension=1, tiled=True)
    return (hidden.astype(jnp.float32) + reduced).astype(jnp.bfloat16)


def slot_table(choices, num_experts):
    experts = jnp.arange(num_experts, dtype=jnp.int32)
    first_hot = (choices[..., 0:1] == experts).astype(jnp.int32)
    second_hot = (choices[..., 1:2] == experts).astype(jnp.int32)
    first_pos = jnp.sum((jnp.cumsum(first_hot, axis=-2) - 1) * first_hot, axis=-1)
    second_base = jnp.cumsum(second_hot, axis=-2) - 1 + jnp.sum(first_hot, axis=-2, keepdims=True)
    second_pos = jnp.sum(second_base * second_hot, axis=-1)
    return jnp.stack([first_pos, second_pos], axis=-1)


def route(normed, choices, w_router, num_experts, capacity):
    logits = jnp.dot(normed.astype(jnp.float32), w_router, precision=lax.Precision.HIGHEST)
    router_probs = jax.nn.softmax(logits, axis=-1)
    picked = jnp.take_along_axis(router_probs, choices, axis=-1)
    gate_weights = picked / jnp.sum(picked, axis=-1, keepdims=True)
    position = slot_table(choices, num_experts)
    slot_ids = jnp.where(position < capacity, choices * capacity + position, -1)
    columns = jnp.arange(num_experts * capacity, dtype=jnp.int32)
    select = (slot_ids[:, :, None] == columns).astype(jnp.bfloat16)
    return gate_weights, select


def moe_block(hidden, ln_scale, w_router, expert_in, expert_out, expert_ids):
    local_batch, local_seq, d_model = hidden.shape
    tokens = local_batch * local_seq
    num_experts = w_router.shape[1]
    local_experts = expert_in.shape[0]
    groups = num_experts // local_experts
    capacity = 4 * tokens // num_experts
    normed = rms_norm(hidden, ln_scale).reshape(tokens, d_model)
    gate_weights, select = route(normed, expert_ids.reshape(tokens, 2), w_router, num_experts, capacity)
    dispatched = jnp.einsum('ncs,nd->sd', select, normed, preferred_element_type=jnp.float32).astype(jnp.bfloat16)
    dispatched = dispatched.reshape(groups, local_experts, capacity, d_model)
    received = lax.all_to_all(dispatched, ('tp', 'ep'), 0, 2, tiled=True)
    expert_rows = received.reshape(local_experts, groups * capacity, d_model)
    expert_hidden = jnp.einsum('erd,edf->erf', expert_rows, expert_in, preferred_element_type=jnp.float32)
    expert_hidden = jax.nn.gelu(expert_hidden).astype(jnp.bfloat16)
    expert_result = jnp.einsum('erf,efd->erd', expert_hidden, expert_out, preferred_element_type=jnp.float32).astype(jnp.bfloat16)
    expert_result = expert_result.reshape(1, local_experts, groups * capacity, d_model)
    returned = lax.all_to_all(expert_result, ('tp', 'ep'), 2, 0, tiled=True)
    returned = returned.reshape(num_experts * capacity, d_model)
    gathered_out = jnp.einsum('ncs,sd->ncd', select, returned, preferred_element_type=jnp.float32)
    moe_sum = jnp.sum(gate_weights[:, :, None] * gathered_out, axis=1).reshape(local_batch, local_seq, d_model)
    return (hidden.astype(jnp.float32) + moe_sum).astype(jnp.bfloat16)


def solution(mesh):
    act_spec = P(('dp', 'ep'), 'tp', None)
    col_spec = P(None, None, 'tp')
    row_spec = P(None, 'tp', None)
    expert_spec = P(('tp', 'ep'), None, None)
    cache_spec = P(None, ('dp', 'ep'), 'tp', None, None)
    in_specs = (act_spec, P(), P(), col_spec, col_spec, col_spec, row_spec, row_spec,
                P(None, 'tp'), P(None, 'tp'), P('tp', None), P(), expert_spec, expert_spec, act_spec)

    def device_fn(hidden_in, ln_attn, ln_ffn, w_query, w_key, w_value, w_out, bias_table, w_gate, w_up, w_down, w_router, expert_in, expert_out, expert_ids):
        hidden, keys_zero, values_zero = attention_block(hidden_in, ln_attn[0], w_query[0], w_key[0], w_value[0], w_out[0], bias_table[0])
        hidden = ffn_block(hidden, ln_ffn[0], w_gate, w_up, w_down)
        hidden, keys_one, values_one = attention_block(hidden, ln_attn[1], w_query[1], w_key[1], w_value[1], w_out[1], bias_table[1])
        hidden = moe_block(hidden, ln_ffn[1], w_router, expert_in, expert_out, expert_ids)
        return hidden, jnp.stack([keys_zero, keys_one]), jnp.stack([values_zero, values_one])

    return jax.shard_map(device_fn, mesh=mesh, in_specs=in_specs, out_specs=(act_spec, cache_spec, cache_spec), check_vma=False)
```

profile of v0, /device:TPU:0, one launch (start us, length us, event | category | flops | bytes accessed | tf_op | source)
XLA Modules:
  0.0 1307.8 jit_solution(12424937701157088665)
XLA Ops:
  10.1 3.5 fusion.23
  14.2 215.5 %gather_fusion.1 = f32[65536,8]{1,0:T(8,128)} fusion(f32[8,32]{0,1:T(8,128)S(1)} %bitcast.180, s32[65536]{0:T(1024)S(1)} %broadcast_clamp_fusion), kind=kCustom, calls=%fused_computation.clone | custom fusion | bytes 4456448 | tf_op jit(solution)/shard_map/jit(_take)/gather | solution.py:27
  229.7 18.7 %copy.149 = f32[256,256,8]{0,1,2:T(8,128)S(1)} copy(f32[256,256,8]{2,1,0:T(8,128)} %bitcast.183) | data formatting | bytes 4194304 | tf_op jit(solution)/shard_map/jit(_take)/gather | solution.py:27
  248.5 215.5 %gather_fusion.2 = f32[65536,8]{1,0:T(8,128)} fusion(f32[8,32]{0,1:T(8,128)S(1)} %bitcast.181, s32[65536]{0:T(1024)S(1)} %broadcast_clamp_fusion), kind=kCustom, calls=%fused_computation.1.clone | custom fusion | bytes 4456448 | tf_op jit(solution)/shard_map/jit(_take)/gather | solution.py:27
  464.0 19.5 %copy.157 = f32[256,256,8]{0,1,2:T(8,128)} copy(f32[256,256,8]{2,1,0:T(8,128)} %bitcast.182) | data formatting | bytes 4194304 | tf_op jit(solution)/shard_map/jit(_take)/gather | solution.py:27
  484.2 4.1 bitcast_select_fusion
  488.4 6.1 convolution_convert_fusion.4
  494.5 2.8 copy.145
  497.4 6.9 convolution_convert_fusion.5
  504.3 3.9 copy.144
  508.2 6.1 convolution_convert_fusion.6
  514.3 3.9 copy.143
  518.3 10.5 fusion.133
  528.7 8.1 fusion.52
  536.9 5.6 fusion.59
  543.2 98.8 %reduce-scatter.4.cloned.1.call-done = f32[8,128,1024]{2,1,0:T(8,128)} async-done(((f32[8,256,1024]{2,1,0:T(8,128)}), f32[8,128,1024]{2,1,0:T(8,128)}) %reduce-scatter.4.cloned.1.call-update) | async-done | bytes 4194320 | tf_op jit(solution)/shard_map/reduce_scatter | solution.py:56
  642.0 2.9 fusion.25
  648.1 54.3 %all-gather.6.cloned.1.call-done = bf16[8,256,1024]{2,1,0:T(8,128)(2,1)} async-done(((bf16[8,128,1024]{2,1,0:T(8,128)(2,1)}), bf16[8,256,1024]{2,1,0:T(8,128)(2,1)}) %all-gather.6.cloned.1.call-update) | async-done | bytes 4194320 | tf_op jit(solution)/shard_map/all_gather | solution.py:62
  702.4 3.6 fusion.79
  706.0 9.7 fusion.53
  715.8 96.5 %reduce-scatter.6.cloned.1.call-done = f32[8,128,1024]{2,1,0:T(8,128)} async-done(((f32[8,256,1024]{2,1,0:T(8,128)}), f32[8,128,1024]{2,1,0:T(8,128)}) %reduce-scatter.6.cloned.1.call-update) | async-done | bytes 4194320 | tf_op jit(solution)/shard_map/reduce_scatter | solution.py:67
  812.3 3.5 fusion.29
  818.2 53.9 %all-gather.8.cloned.1.call-done = bf16[8,256,1024]{2,1,0:T(8,128)(2,1)} async-done(((bf16[8,128,1024]{2,1,0:T(8,128)(2,1)}), bf16[8,256,1024]{2,1,0:T(8,128)(2,1)}) %all-gather.8.cloned.1.call-update) | async-done | bytes 4194320 | tf_op jit(solution)/shard_map/all_gather | solution.py:53
  872.1 6.2 convolution_convert_fusion.1
  878.3 3.9 copy.154
  882.2 6.2 convolution_convert_fusion.3
  888.3 3.9 copy.152
  892.2 6.2 convolution_convert_fusion.2
  898.4 3.9 copy.153
  902.3 10.6 fusion.134
  912.9 8.1 fusion.51
  921.1 5.6 fusion.54
  927.4 9.0 reduce-window.14
  936.8 9.2 reduce-window.16
  946.8 13.8 %convert_reduce_fusion = bf16[1024,4096]{1,0:T(8,128)(2,1)} fusion(s32[1024,2]{0,1:T(2,128)S(1)} %compare_select_fusion.4), kind=kLoop, calls=%fused_computation.5 | loop fusion | flops 29360128 | bytes 8396800 | tf_op jit(solution)/shard_map/ncs,nd->sd/reduce_sum | solution.py:102
  960.6 62.7 %reduce-scatter.8.cloned.1.call-done = f32[8,128,1024]{2,1,0:T(8,128)} async-done(((f32[8,256,1024]{2,1,0:T(8,128)}), f32[8,128,1024]{2,1,0:T(8,128)}) %reduce-scatter.8.cloned.1.call-update) | async-done | bytes 4194320 | tf_op jit(solution)/shard_map/reduce_scatter | solution.py:56
  1023.3 3.0 fusion.33
  1028.7 9.6 fusion.137
  1038.3 96.2 %all_to_all.30 = bf16[8,4,128,1024]{3,2,1,0:T(8,128)(2,1)} all-to-all(bf16[8,4,128,1024]{3,2,1,0:T(8,128)(2,1)S(1)} %bitcast.186), channel_id=1, replica_groups=mesh['dp'=1,'tp'=2,'ep'=4] {'tp','ep'}, dimensions={0} | all-to-all | bytes 16777216 | tf_op jit(solution)/shard_map/all_to_all | solution.py:104
  1134.5 8.2 copy.172
  1142.7 14.9 %convert_bitcast_fusion = bf16[1,4,1024,1024]{3,2,1,0:T(8,128)(2,1)} fusion(bf16[4,512,1024]{2,1,0:T(8,128)(2,1)} %param.30, bf16[4,1024,1024]{2,1,0:T(8,128)(2,1)} %bitcast.187, bf16[4,1024,512]{2,1,0:T(8,128)(2,1)} %param.29), kind=kOutput, calls=%fused_computation.28 | convolution fusion | flops 8613003264 | bytes 25165824 | tf_op jit(solution)/shard_map/erf,efd->erd/dot_general | solution.py:108
  1157.6 12.2 copy.173
  1169.7 3.9 all-to-all-start.1
  1174.2 5.9 pad_maximum_fusion
  1182.1 16.8 %gather_fusion = f32[2048]{0:T(1024)S(1)} fusion(f32[1024,32]{0,1:T(8,128)S(1)} %fusion.106, s32[2048]{0:T(1024)S(1)} %reshape.296), kind=kCustom, calls=%fused_computation.2 | custom fusion | bytes 32768 | tf_op jit(solution)/shard_map/jit(take_along_axis)/gather | solution.py:84
  1200.3 67.3 %all-to-all-done.1 = bf16[1,4,1024,1024]{3,1,0,2:T(4,128)(2,1)} async-done(((bf16[1,4,1024,1024]{3,1,0,2:T(4,128)(2,1)}), bf16[1,4,1024,1024]{3,1,0,2:T(4,128)(2,1)}, u32[]{:S(2)}, u32[]{:S(2)}) %all-to-all-start.1) | async-done | bytes 8388640 | tf_op jit(solution)/shard_map/all_to_all | solution.py:110
  1267.6 9.8 copy.174
  1277.4 21.0 %multiply_reduce_fusion = f32[1024,1024]{1,0:T(8,128)S(1)} fusion(f32[1024,2]{0,1:T(2,128)S(1)} %fusion.108, bf16[4096,1024,1]{1,0,2:T(8,128)(2,1)} %bitcast.185, s32[1024,2]{0,1:T(2,128)S(1)} %copy-done.13), kind=kOutput, calls=%fused_computation.27 | convolution fusion | flops 17191403520 | bytes 12599296 | tf_op jit(solution)/shard_map/ncs,sd->ncd/dot_general | solution.py:112
  (100 shorter events, 20.8 us)
Async XLA Ops:
  7.2 698.8 %copy-start = (bf16[256,1024]{1,0:T(8,128)(2,1)S(1)}, bf16[256,1024]{1,0:T(8,128)(2,1)}, u32[]{:S(2)}) copy-start(bf16[256,1024]{1,0:T(8,128)(2,1)} %param.27) | copy-start | bytes 1572868
  7.2 481.2 %all-gather.4.cloned.1.call-start = ((), (), s32[]{:S(2)}) async-start(), calls=%async_computation.5 | async-start | bytes 6291456 | tf_op jit(solution)/shard_map/all_gather | solution.py:53
  8.0 6.1 copy-start.14
  13.6 628.4 %reduce-scatter.4.cloned.1.call-start = ((), (), s32[]{:S(2)}) async-start(), calls=%async_computation.6 | async-start | bytes 12582912 | tf_op jit(solution)/shard_map/reduce_scatter | solution.py:56
  497.4 20.9 %copy-start.7 = (bf16[8,256,512]{1,2,0:T(8,128)(2,1)}, bf16[8,256,512]{1,2,0:T(8,128)(2,1)S(1)}, u32[]{:S(2)}) copy-start(bf16[8,256,512]{1,2,0:T(8,128)(2,1)S(1)} %copy.145) | copy-start | bytes 6291460
  528.7 8.1 copy-start.16
  542.5 0.7 copy-start.15
  542.5 99.5 %copy-start.2 = (bf16[8,128,1024]{2,1,0:T(8,128)(2,1)S(1)}, bf16[8,128,1024]{2,1,0:T(8,128)(2,1)}, u32[]{:S(2)}) copy-start(bf16[8,128,1024]{2,1,0:T(8,128)(2,1)} %param.17) | copy-start | bytes 6291460
  542.5 159.9 %all-gather.6.cloned.1.call-start = ((), (), s32[]{:S(2)}) async-start(), calls=%async_computation.7 | async-start | bytes 6291456 | tf_op jit(solution)/shard_map/all_gather | solution.py:62
  644.8 1.3 copy-start.5
  648.0 57.9 %copy-start.8 = (bf16[1024,256]{1,0:T(8,128)(2,1)S(1)}, bf16[1024,256]{1,0:T(8,128)(2,1)}, u32[]{:S(2)}) copy-start(bf16[1024,256]{1,0:T(8,128)(2,1)} %param.26) | copy-start | bytes 1572868
  648.0 164.3 %reduce-scatter.6.cloned.1.call-start = ((), (), s32[]{:S(2)}) async-start(), calls=%async_computation.8 | async-start | bytes 12582912 | tf_op jit(solution)/shard_map/reduce_scatter | solution.py:67
  715.7 156.4 %all-gather.8.cloned.1.call-start = ((), (), s32[]{:S(2)}) async-start(), calls=%async_computation.9 | async-start | bytes 6291456 | tf_op jit(solution)/shard_map/all_gather | solution.py:53
  817.8 205.5 %reduce-scatter.8.cloned.1.call-start = ((), (), s32[]{:S(2)}) async-start(), calls=%async_computation.10 | async-start | bytes 12582912 | tf_op jit(solution)/shard_map/reduce_scatter | solution.py:56
  912.9 8.1 copy-start.17
  926.7 0.7 copy-start.9
  946.8 13.8 %copy-start.12 = (s32[1024,2]{0,1:T(2,128)}, s32[1024,2]{0,1:T(2,128)S(1)}, u32[]{:S(2)}) copy-start(s32[1024,2]{0,1:T(2,128)S(1)} %compare_select_fusion.4) | copy-start | bytes 24580
  1023.3 5.4 copy-start.6
  1026.3 1.3 copy-start.3
  1169.7 97.9 %all-to-all-start.1 = ((bf16[1,4,1024,1024]{3,1,0,2:T(4,128)(2,1)}), bf16[1,4,1024,1024]{3,1,0,2:T(4,128)(2,1)}, u32[]{:S(2)}, u32[]{:S(2)}) async-start(bf16[1,4,1024,1024]{3,1,0,2:T(4,128)(2,1)} %copy.173), calls=%async_computation.4 | async-start | bytes 16777216 | tf_op jit(solution)/shard_map/all_to_all | solution.py:110
  1174.2 5.9 copy-start.11
  1182.1 18.1 %copy-start.10 = (s32[8,128,2]{1,2,0:T(2,128)S(1)}, s32[8,128,2]{1,2,0:T(2,128)}, u32[]{:S(2)}) copy-start(s32[8,128,2]{1,2,0:T(2,128)} %param.31) | copy-start | bytes 24580
  1267.6 9.8 copy-start.13
  1277.4 21.0 %copy-start.4 = (bf16[8,128,1024]{2,1,0:T(8,128)(2,1)S(1)}, bf16[8,128,1024]{2,1,0:T(8,128)(2,1)}, u32[]{:S(2)}) copy-start(bf16[8,128,1024]{2,1,0:T(8,128)(2,1)} %copy-done.3) | copy-start | bytes 6291460
  1298.4 2.2 copy-start.1
Sparse Core Ops, SparseCore 0:
  13.7 57.0 all-gather.3
  542.6 99.2 reduce-scatter.3
  648.2 54.1 all-gather.5
  715.8 96.4 reduce-scatter.5
  817.9 54.1 all-gather.7
  926.8 96.4 reduce-scatter.7
where the time goes:
time: 1320 us; the launch traced here: 1310 us
  local copies, waits for them, and re-layouts  547 us (41%)
  waiting for transfers between devices  434 us (33%)
  matrix products  147 us (11%)
  blocking collectives  96.2 us (7%)
  other arithmetic  64.8 us (5%)
  between operations  15 us (1%)
    gather x4, local copies, waits for them, and re-layouts, causal_bias(): bias_full = jnp.take(bias_rows, bucket_of(jnp.maximum(rel_pos, 0)), axis=1)  469 us
    reduce_scatter x2, waiting for transfers between devices, attention_block(): reduced = lax.psum_scatter(part_sum, 'tp', scatter_dimension=1, tiled=True)  161 us
    reduce_scatter x1, waiting for transfers between devices, ffn_block(): reduced = lax.psum_scatter(part_sum, 'tp', scatter_dimension=1, tiled=True)  96.5 us
    all_to_all x1, blocking collectives, moe_block(): received = lax.all_to_all(dispatched, ('tp', 'ep'), 0, 2, tiled=True)  96.2 us
    all_to_all x1, waiting for transfers between devices, moe_block(): returned = lax.all_to_all(expert_result, ('tp', 'ep'), 2, 0, tiled=True)  67.3 us
    all_gather x1, waiting for transfers between devices, ffn_block(): gathered = lax.all_gather(normed, 'tp', axis=1, tiled=True)  54.3 us
    all_gather x2, waiting for transfers between devices, attention_block(): gathered = lax.all_gather(normed, 'tp', axis=1, tiled=True)  53.9 us
    dot_general x6, matrix products, project(): jnp.einsum('btd,dk->btk', normed_full, weight, preferred_element_type=jnp...  37.6 us
  transfers between devices with their start and end apart: 7, of which 6 were waited for; matrix products, arithmetic and copies ran while one was open for 41% of the time, Pallas kernels for 0%

commit v1 on v0

v1 whole, which is shorter than its diff:
```python
import functools

import jax
import jax.numpy as jnp
from jax import lax
from jax.experimental import pallas as pl
from jax.experimental.pallas import tpu as pltpu
from jax.sharding import PartitionSpec as P

EXACT_BUCKETS = 16
THRESHOLDS = (18, 20, 23, 26, 30, 34, 39, 45, 51, 58, 66, 76, 86, 98, 112)
EPSILON = 1e-6
F32 = jnp.float32
BF16 = jnp.bfloat16
TP_SWAP = ((0, 1), (1, 0))
VMEM_LIMIT = 60 * 1024 * 1024


def rms_rows(rows, ln_scale):
    wide = rows.astype(F32)
    inv_rms = lax.rsqrt(jnp.mean(wide * wide, axis=-1, keepdims=True) + EPSILON)
    return (wide * inv_rms * ln_scale).astype(BF16)


def mm(a, b):
    return lax.dot_general(a, b, (((1,), (0,)), ((), ())), preferred_element_type=F32)


def mm_t(a, b):
    return lax.dot_general(a, b, (((1,), (1,)), ((), ())), preferred_element_type=F32)


def fixed(shape, index):
    return pl.BlockSpec(shape, lambda *_: index, pipeline_mode=pl.Buffered(1))


def bias_map(table, seq_len):
    pos = jnp.arange(seq_len, dtype=jnp.int32)
    rel = pos[:, None] - pos[None, :]
    bucket = jnp.minimum(jnp.maximum(rel, 0), EXACT_BUCKETS)
    for threshold in THRESHOLDS:
        bucket = bucket + (rel >= threshold).astype(jnp.int32)
    out = jnp.broadcast_to(table[:, 0][:, None, None], (table.shape[0], seq_len, seq_len))
    for k in range(1, table.shape[1]):
        out = jnp.where(bucket[None] == k, table[:, k][:, None, None], out)
    return jnp.where(rel[None] >= 0, out, -jnp.inf)


def softmax_bf16(scores):
    top = jnp.max(scores, axis=-1, keepdims=True)
    grown = jnp.exp(scores - top)
    return (grown / jnp.sum(grown, axis=-1, keepdims=True)).astype(BF16)


def attention_body(x_ref, ln_ref, wq_ref, wk_ref, wv_ref, w_other_ref, wo_ref, wo_other_ref, bias_ref, out_ref, ctx_ref):
    x = x_ref[0]
    seq_len = x.shape[0]
    half = seq_len // 2
    a = rms_rows(x, ln_ref[0])
    inner = wq_ref.shape[2]
    lanes = lax.broadcasted_iota(jnp.int32, (1, 128), 1)
    first = lanes < 64
    for side in range(2):
        if side == 0:
            q, k, v = (mm(a, ref[0]).astype(BF16) for ref in (wq_ref, wk_ref, wv_ref))
        else:
            q, k, v = (mm(a, w_other_ref[:, i * inner:(i + 1) * inner]).astype(BF16) for i in range(3))
        for pair in range(inner // 128):
            cols = slice(pair * 128, (pair + 1) * 128)
            qp, kp, vp = q[:, cols], k[:, cols], v[:, cols]
            low, high = [], []
            for sub in range(2):
                head = side * (inner // 64) + pair * 2 + sub
                keep = first if sub == 0 else jnp.logical_not(first)
                qh = jnp.where(keep, qp, jnp.zeros_like(qp))
                s_low = mm_t(qh[:half], kp[:half]) * 0.125 + bias_ref[head, :half, :half]
                s_high = mm_t(qh[half:], kp) * 0.125 + bias_ref[head, half:, :]
                low.append(mm(softmax_bf16(s_low), vp[:half]))
                high.append(mm(softmax_bf16(s_high), vp))
            at = side * inner + pair * 128
            ctx_ref[:half, at:at + 128] = jnp.where(first, low[0], low[1]).astype(BF16)
            ctx_ref[half:, at:at + 128] = jnp.where(first, high[0], high[1]).astype(BF16)
    total = mm(ctx_ref[:, :inner], wo_ref[0]) + mm(ctx_ref[:, inner:], wo_other_ref[...])
    out_ref[0] = (x.astype(F32) + total).astype(BF16)


def attention_layer(layer, x, ln, w_query, w_key, w_value, w_other, w_out, wo_other, bias):
    seqs, seq_len, d_model = x.shape
    inner = w_query.shape[2]
    own = fixed((1, d_model, inner), (layer, 0, 0))
    flops = 2 * seqs * seq_len * d_model * (4 * 2 * inner) + 4 * seqs * seq_len * seq_len * 2 * inner
    return pl.pallas_call(
        attention_body,
        grid=(seqs,),
        in_specs=[
            pl.BlockSpec((1, seq_len, d_model), lambda s: (s, 0, 0)),
            fixed((1, d_model), (0, 0)),
            own, own, own,
            fixed(w_other.shape, (0, 0)),
            fixed((1, inner, d_model), (layer, 0, 0)),
            fixed(wo_other.shape, (0, 0)),
            fixed(bias.shape, (0, 0, 0)),
        ],
        out_specs=pl.BlockSpec((1, seq_len, d_model), lambda s: (s, 0, 0)),
        out_shape=jax.ShapeDtypeStruct(x.shape, BF16),
        scratch_shapes=[pltpu.VMEM((seq_len, 2 * inner), BF16)],
        compiler_params=pltpu.CompilerParams(vmem_limit_bytes=VMEM_LIMIT),
        cost_estimate=pl.CostEstimate(flops=flops, bytes_accessed=18 << 20, transcendentals=0),
        name=f"attention{layer}",
    )(x, ln, w_query, w_key, w_value, w_other, w_out, wo_other, bias)


def ffn_body(h_ref, ln_ref, wg_ref, wu_ref, wd_ref, gu_other_ref, wd_other_ref, out_ref):
    h = h_ref[...]
    b = rms_rows(h, ln_ref[0])
    width = wg_ref.shape[1]
    own = (jax.nn.gelu(mm(b, wg_ref[...])) * mm(b, wu_ref[...])).astype(BF16)
    other = (jax.nn.gelu(mm(b, gu_other_ref[:, :width])) * mm(b, gu_other_ref[:, width:])).astype(BF16)
    total = mm(own, wd_ref[...]) + mm(other, wd_other_ref[...])
    out_ref[...] = (h.astype(F32) + total).astype(BF16)


def ffn_layer(rows, ln, w_gate, w_up, w_down, gu_other, wd_other, block=256):
    n, d_model = rows.shape
    flops = 2 * n * d_model * 6 * w_gate.shape[1]
    row_spec = pl.BlockSpec((block, d_model), lambda i: (i, 0))
    weights = [w_gate, w_up, w_down, gu_other, wd_other]
    return pl.pallas_call(
        ffn_body,
        grid=(n // block,),
        in_specs=[row_spec, fixed((1, d_model), (0, 0))] + [fixed(w.shape, (0, 0)) for w in weights],
        out_specs=row_spec,
        out_shape=jax.ShapeDtypeStruct(rows.shape, BF16),
        compiler_params=pltpu.CompilerParams(vmem_limit_bytes=VMEM_LIMIT),
        cost_estimate=pl.CostEstimate(flops=flops, bytes_accessed=7 << 20, transcendentals=0),
        name="ffn",
    )(rows, ln, *weights)


def cache_body(tp_ref, mine_ref, theirs_ref, ln_ref, wk_ref, wv_ref, *rest):
    k_ref, v_ref = rest[-2:]
    step = pl.program_id(0)
    x = jnp.where(step < pl.num_programs(0) // 2, mine_ref[0], theirs_ref[0])
    a = rms_rows(x, ln_ref[0])
    for w_ref, out_ref in ((wk_ref, k_ref), (wv_ref, v_ref)):
        full = mm(a, w_ref[0]).astype(BF16)
        for head in range(out_ref.shape[2]):
            out_ref[0, 0, head] = full[:, head * 64:(head + 1) * 64]


def cache_layer(layer, tp, mine, theirs, ln, w_key, w_value, caches=None):
    half, seq_len, d_model = mine.shape
    inner = w_key.shape[2]
    heads = inner // 64
    shape = jax.ShapeDtypeStruct((2, 2 * half, heads, seq_len, 64), BF16)

    def out_index(t, tp_ref):
        owner = jnp.where(t < half, tp_ref[0], 1 - tp_ref[0])
        return layer, owner * half + lax.rem(t, half), 0, 0, 0

    out_spec = pl.BlockSpec((1, 1, heads, seq_len, 64), out_index)
    own = fixed((1, d_model, inner), (layer, 0, 0))
    in_specs = [
        pl.BlockSpec((1, seq_len, d_model), lambda t, tp_ref: (jnp.minimum(t, half - 1), 0, 0)),
        pl.BlockSpec((1, seq_len, d_model), lambda t, tp_ref: (jnp.maximum(t - half, 0), 0, 0)),
        fixed((1, d_model), (0, 0)), own, own,
    ]
    args = [tp, mine, theirs, ln, w_key, w_value]
    aliases = {}
    if caches is not None:
        in_specs += [pl.BlockSpec(memory_space=pl.ANY)] * 2
        args += list(caches)
        aliases = {6: 0, 7: 1}
    return pl.pallas_call(
        cache_body,
        grid_spec=pltpu.PrefetchScalarGridSpec(
            num_scalar_prefetch=1, grid=(2 * half,), in_specs=in_specs, out_specs=[out_spec, out_spec]),
        out_shape=[shape, shape],
        input_output_aliases=aliases,
        compiler_params=pltpu.CompilerParams(vmem_limit_bytes=VMEM_LIMIT),
        cost_estimate=pl.CostEstimate(flops=8 * half * seq_len * d_model * inner, bytes_accessed=14 << 20, transcendentals=0),
        name=f"cache{layer}",
    )(*args)


def experts_body(dev_ref, h_ref, slot_ref, ln_ref, w_in_ref, w_out_ref, out_ref):
    h = h_ref[...].reshape(-1, h_ref.shape[-1])
    tokens = h.shape[0]
    experts = w_in_ref.shape[0]
    rows = out_ref.shape[1]
    capacity = rows // experts
    want = dev_ref[0] * rows + lax.broadcasted_iota(jnp.int32, (rows, tokens), 0)
    slots = slot_ref[0]
    pick = jnp.logical_or(slots[0:1] == want, slots[1:2] == want)
    chosen = mm(jnp.where(pick, 1.0, 0.0).astype(BF16), h)
    b = rms_rows(chosen, ln_ref[0])
    for e in range(experts):
        at = slice(e * capacity, (e + 1) * capacity)
        hid = jax.nn.gelu(mm(b[at], w_in_ref[e])).astype(BF16)
        out_ref[0, at] = mm(hid, w_out_ref[e]).astype(BF16)


def experts_layer(dev, h_all, slots, ln, expert_in, expert_out):
    tp_n, ep_n, seqs, _, positions, d_model = h_all.shape
    experts = expert_in.shape[0]
    tokens = tp_n * seqs * positions
    groups = tp_n * ep_n
    rows = experts * (4 * tokens // (experts * groups))
    flops = groups * 2 * rows * d_model * (tokens + 2 * expert_in.shape[2])
    return pl.pallas_call(
        experts_body,
        grid_spec=pltpu.PrefetchScalarGridSpec(
            num_scalar_prefetch=1,
            grid=(groups,),
            in_specs=[
                pl.BlockSpec((tp_n, 1, seqs, 1, positions, d_model), lambda g, d: (0, g % ep_n, 0, g // ep_n, 0, 0)),
                pl.BlockSpec((1, 2, tokens), lambda g, d: (g, 0, 0)),
                fixed((1, d_model), (0, 0)),
                fixed(expert_in.shape, (0, 0, 0)),
                fixed(expert_out.shape, (0, 0, 0)),
            ],
            out_specs=pl.BlockSpec((1, rows, d_model), lambda g, d: (g, 0, 0)),
        ),
        out_shape=jax.ShapeDtypeStruct((groups, rows, d_model), BF16),
        compiler_params=pltpu.CompilerParams(vmem_limit_bytes=VMEM_LIMIT),
        cost_estimate=pl.CostEstimate(flops=flops, bytes_accessed=32 << 20, transcendentals=0),
        name="experts",
    )(dev, h_all, slots, ln, expert_in, expert_out)


def combine_body(h_ref, slot_ref, gate_ref, rows_ref, out_ref):
    block = h_ref.shape[0]
    total = rows_ref.shape[0]
    columns = lax.broadcasted_iota(jnp.int32, (block, total), 1)
    out = h_ref[...].astype(F32)
    parts = []
    for c in range(2):
        pick = jnp.where(slot_ref[:, c:c + 1] == columns, 1.0, 0.0).astype(BF16)
        parts.append(gate_ref[:, c:c + 1] * mm(pick, rows_ref[...]))
    out_ref[...] = (out + (parts[0] + parts[1])).astype(BF16)


def combine_layer(h, slots, gates, rows, block=128):
    n, d_model = h.shape
    total = rows.shape[0]
    return pl.pallas_call(
        combine_body,
        grid=(n // block,),
        in_specs=[
            pl.BlockSpec((block, d_model), lambda i: (i, 0)),
            pl.BlockSpec((block, 2), lambda i: (i, 0)),
            pl.BlockSpec((block, 2), lambda i: (i, 0)),
            fixed(rows.shape, (0, 0)),
        ],
        out_specs=pl.BlockSpec((block, d_model), lambda i: (i, 0)),
        out_shape=jax.ShapeDtypeStruct(h.shape, BF16),
        compiler_params=pltpu.CompilerParams(vmem_limit_bytes=VMEM_LIMIT),
        cost_estimate=pl.CostEstimate(flops=4 * n * total * d_model, bytes_accessed=13 << 20, transcendentals=0),
        name="combine",
    )(h, slots, gates, rows)


def slot_table(choices, num_experts, capacity):
    tokens = choices.shape[0]
    experts = jnp.arange(num_experts, dtype=jnp.int32)
    hot = (choices[:, :, None] == experts).astype(BF16).reshape(tokens, 2 * num_experts)
    rows = jnp.arange(tokens, dtype=jnp.int32)
    tri = (rows[:, None] >= rows[None, :]).astype(BF16)
    upto = mm(tri, hot)
    wide = hot.astype(F32)
    first_hot, second_hot = wide[:, :num_experts], wide[:, num_experts:]
    first_pos = jnp.sum((upto[:, :num_experts] - 1.0) * first_hot, axis=-1)
    base = upto[-1:, :num_experts] - 1.0
    second_pos = jnp.sum((upto[:, num_experts:] + base) * second_hot, axis=-1)
    position = jnp.stack([first_pos, second_pos], axis=-1).astype(jnp.int32)
    return jnp.where(position < capacity, choices * capacity + position, -1)


def solution(mesh):
    act_spec = P(('dp', 'ep'), 'tp', None)
    col_spec = P(None, None, 'tp')
    row_spec = P(None, 'tp', None)
    expert_spec = P(('tp', 'ep'), None, None)
    cache_spec = P(None, ('dp', 'ep'), 'tp', None, None)
    in_specs = (act_spec, P(), P(), col_spec, col_spec, col_spec, row_spec, row_spec,
                P(None, 'tp'), P(None, 'tp'), P('tp', None), P(), expert_spec, expert_spec, act_spec)
    tp_n, ep_n = mesh.shape['tp'], mesh.shape['ep']

    def device_fn(hidden_in, ln_attn, ln_ffn, w_query, w_key, w_value, w_out, bias_table, w_gate, w_up, w_down, w_router, expert_in, expert_out, expert_ids):
        batch, positions, d_model = hidden_in.shape
        half = batch // 2
        tp, ep = lax.axis_index('tp'), lax.axis_index('ep')
        swap = lambda value: lax.ppermute(value, 'tp', TP_SWAP)
        spread = lambda value: lax.all_gather(value, 'ep', axis=0, tiled=False)

        def quarter(weight):
            rows = weight.shape[0] // ep_n
            return lax.dynamic_slice_in_dim(weight, ep * rows, rows, 0)

        def whole_seq(own, other):
            return jnp.where(tp == 0, jnp.concatenate([own, other], axis=1), jnp.concatenate([other, own], axis=1))

        def qkv_other(layer):
            part = jnp.concatenate([quarter(w[layer]) for w in (w_query, w_key, w_value)], axis=1)
            return spread(swap(part)).reshape(d_model, -1)

        kept = lax.dynamic_slice_in_dim(hidden_in, tp * half, half, 0)
        given = lax.dynamic_slice_in_dim(hidden_in, (1 - tp) * half, half, 0)

        wqkv0 = qkv_other(0)
        x0 = whole_seq(kept, swap(given))
        out_part0 = quarter(w_out[0])
        down_part = quarter(w_down)
        gu_part = jnp.concatenate([quarter(w_gate), quarter(w_up)], axis=1)
        tail0 = jnp.concatenate([out_part0, down_part, gu_part.reshape(-1, d_model)], axis=0)
        tail0 = spread(swap(tail0))
        n_out, n_down = out_part0.shape[0], down_part.shape[0]
        wo0 = tail0[:, :n_out].reshape(-1, d_model)
        wd_other = tail0[:, n_out:n_out + n_down].reshape(-1, d_model)
        gu_other = tail0[:, n_out + n_down:].reshape(d_model, -1)
        wqkv1 = qkv_other(1)
        wo1 = spread(swap(quarter(w_out[1]))).reshape(-1, d_model)
        bias_all = jnp.concatenate([bias_table, swap(bias_table)], axis=1)

        num_experts = w_router.shape[1]
        tokens = batch * positions
        capacity = 4 * tokens // num_experts
        choices = expert_ids.reshape(tokens, 2)
        slots = slot_table(choices, num_experts, capacity)
        slots_all = lax.all_gather(slots.T, ('tp', 'ep'), axis=0, tiled=False)

        h = attention_layer(0, x0, ln_attn[0:1], w_query, w_key, w_value, wqkv0, w_out, wo0, bias_map(bias_all[0], tp_n * positions))
        h1 = ffn_layer(h.reshape(tokens, d_model), ln_ffn[0:1], w_gate, w_up, w_down, gu_other, wd_other).reshape(h.shape)
        h2 = attention_layer(1, h1, ln_attn[1:2], w_query, w_key, w_value, wqkv1, w_out, wo1, bias_map(bias_all[1], tp_n * positions))

        tp_arr = tp.reshape(1).astype(jnp.int32)
        x0_theirs = whole_seq(given, swap(kept))
        caches = cache_layer(0, tp_arr, x0, x0_theirs, ln_attn[0:1], w_key, w_value)
        k_cache, v_cache = cache_layer(1, tp_arr, h1, swap(h1), ln_attn[1:2], w_key, w_value, caches)

        h_all = lax.all_gather(h2, ('tp', 'ep'), axis=0, tiled=False)
        h_all = h_all.reshape(tp_n, ep_n, half, tp_n, positions, d_model)
        dev = (tp * ep_n + ep).reshape(1).astype(jnp.int32)
        results = experts_layer(dev, h_all, slots_all, ln_ffn[1:2], expert_in, expert_out)
        returned = lax.all_to_all(results, ('tp', 'ep'), 0, 0, tiled=True).reshape(num_experts * capacity, d_model)

        h_own = lax.dynamic_slice(h_all, (0, ep, 0, tp, 0, 0), (tp_n, 1, half, 1, positions, d_model)).reshape(tokens, d_model)
        b = rms_rows(h_own, ln_ffn[1])
        logits = jnp.dot(b.astype(F32), w_router, precision=lax.Precision.HIGHEST)
        probs = jax.nn.softmax(logits, axis=-1)
        hot = choices[:, :, None] == jnp.arange(num_experts, dtype=jnp.int32)
        picked = jnp.sum(jnp.where(hot, probs[:, None, :], 0.0), axis=-1)
        gates = picked / jnp.sum(picked, axis=-1, keepdims=True)
        hidden = combine_layer(h_own, slots, gates, returned).reshape(hidden_in.shape)
        return hidden, k_cache, v_cache

    return jax.shard_map(device_fn, mesh=mesh, in_specs=in_specs, out_specs=(act_spec, cache_spec, cache_spec), check_vma=False)
```

time: 1320 us -> 601 us (0.46)
  local copies, waits for them, and re-layouts: 547 us -> 47.6 us
  Pallas kernels: 0 us -> 158 us
  waiting for transfers between devices: 434 us -> 280 us
  matrix products: 147 us -> 2.54 us
  blocking collectives: 96.2 us -> 11.8 us
    gather x11 -> x0, local copies, waits for them, and re-layouts: 488 us -> none  [the longest x4 469 us: causal_bias(): bias_full = jnp.take(bias_rows, bucket_of(jnp.maximum(rel_pos, 0)), axis=1)]
    reduce_scatter x3 -> x0, waiting for transfers between devices: 258 us -> none  [the longest x2 161 us: attention_block(): reduced = lax.psum_scatter(part_sum, 'tp', scatter_dimension=1, tiled=True)]
    ppermute x0 -> x8, waiting for transfers between devices: none -> 211 us  [device_fn(): swap = lambda value: lax.ppermute(value, 'tp', TP_SWAP)]
    pallas_call x0 -> x7, Pallas kernels: none -> 158 us  [the longest x2 73.3 us: attention_layer(): pl.pallas_call(attention_body, grid=(seqs,), in_specs=[pl.BlockSpec((1, s...]
    dot_general x16 -> x2, matrix products: 126 us -> 2.54 us  [the longest x1 1.96 us: device_fn(): logits = jnp.dot(b.astype(F32), w_router, precision=lax.Precision.HIGHEST)]
    all_to_all x1 -> x0, blocking collectives: 96.2 us -> none  [moe_block(): received = lax.all_to_all(dispatched, ('tp', 'ep'), 0, 2, tiled=True)]
    all_to_all x1, waiting for transfers between devices: 67.3 us -> 0.01 us  [device_fn(): lax.all_to_all(results, ('tp', 'ep'), 0, 0, tiled=True)]
    select_n x2 -> x5, other arithmetic: 4.13 us -> 47.2 us  [the longest x2 39.8 us: bias_map(): return jnp.where(rel[None] >= 0, out, -jnp.inf)]
  transfers between devices with their start and end apart: 7 -> 14, of which waited for: 6 -> 6; matrix products, arithmetic and copies ran while one was open for 41% -> 18% of each run, Pallas kernels for 0% -> 11%
where the time goes in v1:
time: 601 us; the launch traced here: 594 us
  waiting for transfers between devices  280 us (47%)
  Pallas kernels  158 us (26%)
  other arithmetic  63.7 us (11%)
  local copies, waits for them, and re-layouts  47.6 us (8%)
  starting transfers between devices  15.7 us (3%)
  between operations  15 us (2%)
  blocking collectives  11.8 us (2%)
    ppermute x8, waiting for transfers between devices, device_fn(): swap = lambda value: lax.ppermute(value, 'tp', TP_SWAP)  211 us
    pallas_call x2, Pallas kernels, attention_layer(): pl.pallas_call(attention_body, grid=(seqs,), in_specs=[pl.BlockSpec((1, s...  73.3 us
    all_gather x1, waiting for transfers between devices, device_fn(): h_all = lax.all_gather(h2, ('tp', 'ep'), axis=0, tiled=False)  68.8 us
    select_n x2, other arithmetic, bias_map(): return jnp.where(rel[None] >= 0, out, -jnp.inf)  39.8 us
    pallas_call x1, Pallas kernels, experts_layer(): pl.pallas_call(experts_body, grid_spec=pltpu.PrefetchScalarGridSpec(num_s...  30.4 us
    pallas_call x1, Pallas kernels, combine_layer(): pl.pallas_call(combine_body, grid=(n // block,), in_specs=[pl.BlockSpec((...  23.7 us
    pallas_call x2, Pallas kernels, cache_layer(): pl.pallas_call(cache_body, grid_spec=pltpu.PrefetchScalarGridSpec(num_sca...  22.8 us
    unnamed x107, local copies, waits for them, and re-layouts  21 us
  transfers between devices with their start and end apart: 14, of which 6 were waited for; matrix products, arithmetic and copies ran while one was open for 18% of the time, Pallas kernels for 11%

profile of v1, /device:TPU:0, one launch (start us, length us, event | category | flops | bytes accessed | tf_op | source)
XLA Modules:
  0.0 594.3 jit_solution(6004742633302563447)
XLA Ops:
  7.2 1.0 constant_dynamic-slice_fusion.1
  8.4 1.7 fusion.26
  11.1 3.4 collective-permute-start.2
  14.5 14.7 %collective-permute-done.2 = bf16[320,1024]{1,0:T(8,128)(2,1)S(1)} collective-permute-done((bf16[320,1024]{1,0:T(8,128)(2,1)S(1)}, bf16[320,1024]{1,0:T(8,128)(2,1)S(1)}, u32[]{:S(2)}, u32[]{:S(2)}) %collective-permute-start.2) | collective-permute-done | bytes 655392 | tf_op jit(solution)/shard_map/ppermute | solution.py:293
  30.2 2.8 fusion.27
  33.0 1.1 fusion.28
  34.1 1.1 fusion.29
  35.3 1.8 collective-permute-start.1
  37.1 17.0 %collective-permute-done.1 = bf16[256,1536]{1,0:T(8,128)(2,1)S(1)} collective-permute-done((bf16[256,1536]{1,0:T(8,128)(2,1)S(1)}, bf16[256,1536]{1,0:T(8,128)(2,1)S(1)}, u32[]{:S(2)}, u32[]{:S(2)}) %collective-permute-start.1) | collective-permute-done | bytes 786464 | tf_op jit(solution)/shard_map/ppermute | solution.py:293
  55.0 1.5 collective-permute-start.3
  56.5 1.8 constant_dynamic-slice_fusion.5
  59.0 1.5 collective-permute-start.5
  60.4 1.0 dynamic-slice_bitcast_fusion.3
  61.4 1.1 dynamic-slice_bitcast_fusion.1
  62.5 0.9 pad_maximum_fusion.1
  74.0 16.0 %collective-permute-done.5 = bf16[128,1024]{1,0:T(8,128)(2,1)} collective-permute-done((bf16[128,1024]{1,0:T(8,128)(2,1)S(1)}, bf16[128,1024]{1,0:T(8,128)(2,1)}, u32[]{:S(2)}, u32[]{:S(2)}) %collective-permute-start.5) | collective-permute-done | bytes 262176 | tf_op jit(solution)/shard_map/ppermute | solution.py:293
  94.5 1.0 slice_reduce_fusion.30
  95.4 1.0 slice_reduce_fusion.62
  96.4 1.1 slice_reduce_fusion.31
  97.5 1.0 slice_reduce_fusion.63
  98.5 5.3 collective-permute-done.4
  103.9 1.0 copy-done.6
  105.4 20.1 %select_select_fusion.bias_ref = f32[16,256,256]{2,1,0:T(8,128)} fusion(f32[16]{0:T(128)} %get-tuple-element.28, f32[16]{0:T(128)} %get-tuple-element.29, f32[16]{0:T(128)} %get-tuple-element.30, f32[16]{0:T(128)} %get-tuple-element.31, f32[16]{0:T(128)} %get-tuple-element.32, f32[16]{0:T(128)} %get-tuple-element.33, f32[16]{0:T(128)} %get-tuple-element.34, ...), kind=kLoop, calls=%fused_computation.3 | loop fusion | flops 33554432 | bytes 6293504 | tf_op jit(solution)/shard_map/jit(_where)/select_n | solution.py:46
  126.0 19.7 %select_select_fusion.1.bias_ref = f32[16,256,256]{2,1,0:T(8,128)} fusion(f32[16]{0:T(128)S(1)} %copy-done.46, f32[16]{0:T(128)S(1)} %copy-done.47, f32[16]{0:T(128)S(1)} %copy-done.48, f32[16]{0:T(128)S(1)} %copy-done.49, f32[16]{0:T(128)S(1)} %copy-done.50, f32[16]{0:T(128)} %get-tuple-element.65, f32[16]{0:T(128)} %get-tuple-element.66, ...), kind=kLoop, calls=%fused_computation.4 | loop fusion | flops 33554432 | bytes 6293504 | tf_op jit(solution)/shard_map/jit(_where)/select_n | solution.py:46
  145.7 4.0 maximum_select_fusion.x_ref.mine_ref
  149.6 1.9 slice.382
  151.5 2.9 fusion.25
  154.4 1.2 reshape.558.gu_other_ref
  155.7 36.5 %attention0.1 = bf16[4,256,1024]{2,1,0:T(8,128)(2,1)} custom-call(bf16[4,256,1024]{2,1,0:T(8,128)(2,1)} %maximum_select_fusion.x_ref.mine_ref, f32[1,1024]{1,0:T(1,128)} %get-tuple-element.112.ln_ref, bf16[2,1024,512]{2,1,0:T(8,128)(2,1)} %wq_ref.3, bf16[2,1024,512]{2,1,0:T(8,128)(2,1)} %wk_ref.7, bf16[2,1024,512]{2,1,0:T(8,128)(2,1)} %wv_ref.7, ...), custom_call_target="tpu_custom_call" | custom-call | flops 9663676416 | bytes 18874368 | tf_op jit(solution)/shard_map/attention0/pallas_call | solution.py:92
  192.2 7.7 %ffn.1 = bf16[1024,1024]{1,0:T(8,128)(2,1)} custom-call(bf16[1024,1024]{1,0:T(8,128)(2,1)} %bitcast.66, f32[1,1024]{1,0:T(1,128)} %get-tuple-element.110.ln_ref, bf16[1024,256]{1,0:T(8,128)(2,1)} %wg_ref.1, bf16[1024,256]{1,0:T(8,128)(2,1)} %wu_ref.1, bf16[256,1024]{1,0:T(8,128)(2,1)} %wd_ref.1, bf16[1024,512]{1,0:T(8,128)(2,1)} %reshape.558.gu_other_ref, ...), custom_call_target="tpu_custom_call" | custom-call | flops 3221225472 | bytes 7340032 | tf_op jit(solution)/shard_map/ffn/pallas_call | solution.py:128
  199.8 36.8 %attention1.1 = bf16[4,256,1024]{2,1,0:T(8,128)(2,1)} custom-call(bf16[4,256,1024]{2,1,0:T(8,128)(2,1)} %bitcast.49, f32[1,1024]{1,0:T(1,128)} %get-tuple-element.111.ln_ref, bf16[2,1024,512]{2,1,0:T(8,128)(2,1)} %wq_ref.3, bf16[2,1024,512]{2,1,0:T(8,128)(2,1)} %wk_ref.7, bf16[2,1024,512]{2,1,0:T(8,128)(2,1)} %wv_ref.7, ...), custom_call_target="tpu_custom_call" | custom-call | flops 9663676416 | bytes 18874368 | tf_op jit(solution)/shard_map/attention1/pallas_call | solution.py:92
  238.5 1.0 copy.44
  239.5 1.1 add_select_fusion.slot_ref
  240.9 11.8 %all-gather.6.slot_ref = s32[8,2,1024]{2,1,0:T(2,128)} all-gather(s32[1,2,1024]{2,1,0:T(2,128)S(1)} %copy.48), channel_id=7, replica_groups=mesh['dp'=1,'tp'=2,'ep'=4] {'tp','ep'}, dimensions={0}, use_global_device_ids=true | all-gather | bytes 73728 | tf_op jit(solution)/shard_map/all_gather | solution.py:330
  252.7 68.8 %all-gather.21.cloned.1.call-done = bf16[32,256,1024]{2,1,0:T(8,128)(2,1)} async-done(((bf16[4,256,1024]{2,1,0:T(8,128)(2,1)}), bf16[32,256,1024]{2,1,0:T(8,128)(2,1)}) %all-gather.21.cloned.1.call-update) | async-done | bytes 16777232 | tf_op jit(solution)/shard_map/all_gather | solution.py:341
  321.5 30.4 %experts.1 = bf16[8,512,1024]{2,1,0:T(8,128)(2,1)} custom-call(s32[1]{0:T(128)} %bitcast.23.dev_ref, bf16[2,4,4,2,128,1024]{5,4,3,2,1,0:T(8,128)(2,1)} %bitcast.57, s32[8,2,1024]{2,1,0:T(2,128)} %all-gather.6.slot_ref, f32[1,1024]{1,0:T(1,128)} %get-tuple-element.109.ln_ref, bf16[4,1024,512]{2,1,0:T(8,128)(2,1)} %w_in_ref.1, bf16[4,512,1024]{2,1,0:T(8,128)(2,1)} %w_out_ref.1), custom_call_target="tpu_custom_call" | custom-call | flops 17179869184 | bytes 33554432 | tf_op jit(solution)/shard_map/experts/pallas_call | solution.py:210
  351.9 4.0 all-to-all-start
  355.9 2.0 collective-permute-start.6
  358.0 158.1 %collective-permute-done.7 = bf16[4,128,1024]{2,1,0:T(8,128)(2,1)S(1)} collective-permute-done((bf16[4,128,1024]{2,1,0:T(8,128)(2,1)S(1)}, bf16[4,128,1024]{2,1,0:T(8,128)(2,1)S(1)}, u32[]{:S(2)}, u32[]{:S(2)}) %collective-permute-start.7) | collective-permute-done | bytes 1048608 | tf_op jit(solution)/shard_map/ppermute | solution.py:293
  516.1 2.3 maximum_select_fusion.1.theirs_ref
  518.4 11.4 %cache0.1 = (bf16[2,8,8,256,64]{4,3,2,1,0:T(8,128)(2,1)}, bf16[2,8,8,256,64]{4,3,2,1,0:T(8,128)(2,1)}) custom-call(s32[1]{0:T(128)} %bitcast.28.tp_ref, bf16[4,256,1024]{2,1,0:T(8,128)(2,1)} %maximum_select_fusion.x_ref.mine_ref, bf16[4,256,1024]{2,1,0:T(8,128)(2,1)} %maximum_select_fusion.1.theirs_ref, f32[1,1024]{1,0:T(1,128)} %get-tuple-element.112.ln_ref, ...), custom_call_target="tpu_custom_call" | custom-call | flops 4294967296 | bytes 14680064 | tf_op jit(solution)/shard_map/cache0/pallas_call | solution.py:174
  529.8 11.4 %cache1.1 = (bf16[2,8,8,256,64]{4,3,2,1,0:T(8,128)(2,1)}, bf16[2,8,8,256,64]{4,3,2,1,0:T(8,128)(2,1)}) custom-call(s32[1]{0:T(128)} %bitcast.28.tp_ref, bf16[4,256,1024]{2,1,0:T(8,128)(2,1)} %bitcast.51, bf16[4,256,1024]{2,1,0:T(8,128)(2,1)} %collective-permute-done.6.theirs_ref, ...), custom_call_target="tpu_custom_call", output_to_operand_aliasing={{0}: (6, {}), {1}: (7, {})} | custom-call | flops 4294967296 | bytes 14680064 | tf_op jit(solution)/shard_map/cache1/pallas_call | solution.py:174
  541.2 8.5 %copy.49 = bf16[2,8,8,256,64]{3,4,2,1,0:T(8,128)(2,1)} copy(bf16[2,8,8,256,64]{4,3,2,1,0:T(8,128)(2,1)} %get-tuple-element.21) | data formatting | bytes 8388608
  549.7 8.5 %copy.50 = bf16[2,8,8,256,64]{3,4,2,1,0:T(8,128)(2,1)} copy(bf16[2,8,8,256,64]{4,3,2,1,0:T(8,128)(2,1)} %get-tuple-element.22) | data formatting | bytes 8388608
  558.3 2.1 multiply_reduce_fusion
  560.4 2.0 fusion.32
  562.7 1.0 broadcast_divide_fusion.gate_ref
  563.7 23.7 %combine.1 = bf16[1024,1024]{1,0:T(8,128)(2,1)} custom-call(bf16[1024,1024]{1,0:T(8,128)(2,1)} %bitcast.53, s32[1024,2]{1,0:T(8,128)} %copy-done.4, f32[1024,2]{1,0:T(8,128)} %broadcast_divide_fusion.gate_ref, bf16[4096,1024]{1,0:T(8,128)(2,1)} %bitcast.26.rows_ref), custom_call_target="tpu_custom_call" | custom-call | flops 17179869184 | bytes 13631488 | tf_op jit(solution)/shard_map/combine/pallas_call | solution.py:246
  (169 shorter events, 21.6 us)
Async XLA Ops:
  7.2 553.2 %copy-start = (f32[1024,32]{0,1:T(8,128)S(1)}, f32[1024,32]{0,1:T(8,128)}, u32[]{:S(2)}) copy-start(f32[1024,32]{0,1:T(8,128)} %param.26) | copy-start | bytes 393220
  7.2 142.4 %all-gather.15.cloned.1.call-start = ((), (), s32[]{:S(2)}) async-start(), calls=%async_computation.2 | async-start | bytes 3276800 | tf_op jit(solution)/shard_map/all_gather | solution.py:294
  11.1 18.1 %collective-permute-start.2 = (bf16[320,1024]{1,0:T(8,128)(2,1)S(1)}, bf16[320,1024]{1,0:T(8,128)(2,1)S(1)}, u32[]{:S(2)}, u32[]{:S(2)}) collective-permute-start(bf16[320,1024]{1,0:T(8,128)(2,1)S(1)} %pad_maximum_fusion.2), channel_id=1, source_target_pairs={{0,4},{4,0},{1,5},{5,1},{2,6},{6,2},{3,7},{7,3}} | collective-permute-start | bytes 1966088 | tf_op jit(solution)/shard_map/ppermute | solution.py:293
  30.1 125.5 %all-gather.13.cloned.1.call-start = ((), (), s32[]{:S(2)}) async-start(), calls=%async_computation.1 | async-start | bytes 3932160 | tf_op jit(solution)/shard_map/all_gather | solution.py:294
  35.3 18.7 %collective-permute-start.1 = (bf16[256,1536]{1,0:T(8,128)(2,1)S(1)}, bf16[256,1536]{1,0:T(8,128)(2,1)S(1)}, u32[]{:S(2)}, u32[]{:S(2)}) collective-permute-start(bf16[256,1536]{1,0:T(8,128)(2,1)S(1)} %pad_maximum_fusion), channel_id=1, source_target_pairs={{0,4},{4,0},{1,5},{5,1},{2,6},{6,2},{3,7},{7,3}} | collective-permute-start | bytes 2359304 | tf_op jit(solution)/shard_map/ppermute | solution.py:293
  55.0 144.9 %all-gather.19.cloned.1.call-start = ((), (), s32[]{:S(2)}) async-start(), calls=%async_computation.4 | async-start | bytes 1310720 | tf_op jit(solution)/shard_map/all_gather | solution.py:294
  55.0 38.8 %collective-permute-start.3 = (f32[2,8,32]{2,1,0:T(8,128)}, f32[2,8,32]{2,1,0:T(8,128)}, u32[]{:S(2)}, u32[]{:S(2)}) collective-permute-start(f32[2,8,32]{2,1,0:T(8,128)} %param.22), channel_id=1, source_target_pairs={{0,4},{4,0},{1,5},{5,1},{2,6},{6,2},{3,7},{7,3}} | collective-permute-start | bytes 6152 | tf_op jit(solution)/shard_map/ppermute | solution.py:293
  56.5 35.4 %copy-start.33 = (f32[2,1024]{1,0:T(2,128)S(1)}, f32[2,1024]{1,0:T(2,128)}, u32[]{:S(2)}) copy-start(f32[2,1024]{1,0:T(2,128)} %param.16) | copy-start | bytes 24580
  56.5 36.0 %copy-start.34 = (f32[2,1024]{1,0:T(2,128)S(1)}, f32[2,1024]{1,0:T(2,128)}, u32[]{:S(2)}) copy-start(f32[2,1024]{1,0:T(2,128)} %param.17) | copy-start | bytes 24580
  58.3 87.3 %collective-permute-start = (bf16[4,128,1024]{2,1,0:T(8,128)(2,1)S(1)}, bf16[4,128,1024]{2,1,0:T(8,128)(2,1)}, u32[]{:S(2)}, u32[]{:S(2)}) collective-permute-start(bf16[4,128,1024]{2,1,0:T(8,128)(2,1)S(1)} %get-tuple-element.104), channel_id=1, source_target_pairs={{0,4},{4,0},{1,5},{5,1},{2,6},{6,2},{3,7},{7,3}} | collective-permute-start | bytes 3145736 | tf_op jit(solution)/shard_map/ppermute | solution.py:293
  59.0 31.1 %collective-permute-start.5 = (bf16[128,1024]{1,0:T(8,128)(2,1)S(1)}, bf16[128,1024]{1,0:T(8,128)(2,1)}, u32[]{:S(2)}, u32[]{:S(2)}) collective-permute-start(bf16[128,1024]{1,0:T(8,128)(2,1)S(1)} %dynamic-slice_bitcast_fusion), channel_id=1, source_target_pairs={{0,4},{4,0},{1,5},{5,1},{2,6},{6,2},{3,7},{7,3}} | collective-permute-start | bytes 786440 | tf_op jit(solution)/shard_map/ppermute | solution.py:293
  63.4 40.4 %collective-permute-start.4 = (bf16[256,1536]{1,0:T(8,128)(2,1)}, bf16[256,1536]{1,0:T(8,128)(2,1)S(1)}, u32[]{:S(2)}, u32[]{:S(2)}) collective-permute-start(bf16[256,1536]{1,0:T(8,128)(2,1)} %pad_maximum_fusion.1), channel_id=1, source_target_pairs={{0,4},{4,0},{1,5},{5,1},{2,6},{6,2},{3,7},{7,3}} | collective-permute-start | bytes 2359304 | tf_op jit(solution)/shard_map/ppermute | solution.py:293
  90.0 109.8 %all-gather.17.cloned.1.call-start = ((), (), s32[]{:S(2)}) async-start(), calls=%async_computation.3 | async-start | bytes 3932160 | tf_op jit(solution)/shard_map/all_gather | solution.py:294
  104.8 20.7 %copy-start.8 = (pred[256,256]{1,0:T(8,128)(4,1)S(1)}, pred[256,256]{1,0:T(8,128)(4,1)}, u32[]{:S(2)}) copy-start(pred[256,256]{1,0:T(8,128)(4,1)} %get-tuple-element.143) | copy-start | bytes 196612
  104.8 20.7 %copy-start.9 = (pred[256,256]{1,0:T(8,128)(4,1)S(1)}, pred[256,256]{1,0:T(8,128)(4,1)}, u32[]{:S(2)}) copy-start(pred[256,256]{1,0:T(8,128)(4,1)} %get-tuple-element.144) | copy-start | bytes 196612
  104.9 20.7 %copy-start.10 = (pred[256,256]{1,0:T(8,128)(4,1)S(1)}, pred[256,256]{1,0:T(8,128)(4,1)}, u32[]{:S(2)}) copy-start(pred[256,256]{1,0:T(8,128)(4,1)} %get-tuple-element.141) | copy-start | bytes 196612
  104.9 20.7 %copy-start.11 = (pred[256,256]{1,0:T(8,128)(4,1)S(1)}, pred[256,256]{1,0:T(8,128)(4,1)}, u32[]{:S(2)}) copy-start(pred[256,256]{1,0:T(8,128)(4,1)} %get-tuple-element.142) | copy-start | bytes 196612
  104.9 20.7 %copy-start.12 = (pred[256,256]{1,0:T(8,128)(4,1)S(1)}, pred[256,256]{1,0:T(8,128)(4,1)}, u32[]{:S(2)}) copy-start(pred[256,256]{1,0:T(8,128)(4,1)} %get-tuple-element.139) | copy-start | bytes 196612
  104.9 20.7 %copy-start.13 = (pred[256,256]{1,0:T(8,128)(4,1)S(1)}, pred[256,256]{1,0:T(8,128)(4,1)}, u32[]{:S(2)}) copy-start(pred[256,256]{1,0:T(8,128)(4,1)} %get-tuple-element.140) | copy-start | bytes 196612
  104.9 20.7 %copy-start.14 = (pred[256,256]{1,0:T(8,128)(4,1)S(1)}, pred[256,256]{1,0:T(8,128)(4,1)}, u32[]{:S(2)}) copy-start(pred[256,256]{1,0:T(8,128)(4,1)} %get-tuple-element.137) | copy-start | bytes 196612
  104.9 20.7 %copy-start.15 = (pred[256,256]{1,0:T(8,128)(4,1)S(1)}, pred[256,256]{1,0:T(8,128)(4,1)}, u32[]{:S(2)}) copy-start(pred[256,256]{1,0:T(8,128)(4,1)} %get-tuple-element.138) | copy-start | bytes 196612
  104.9 20.7 %copy-start.16 = (pred[256,256]{1,0:T(8,128)(4,1)S(1)}, pred[256,256]{1,0:T(8,128)(4,1)}, u32[]{:S(2)}) copy-start(pred[256,256]{1,0:T(8,128)(4,1)} %get-tuple-element.135) | copy-start | bytes 196612
  104.9 20.7 %copy-start.17 = (pred[256,256]{1,0:T(8,128)(4,1)S(1)}, pred[256,256]{1,0:T(8,128)(4,1)}, u32[]{:S(2)}) copy-start(pred[256,256]{1,0:T(8,128)(4,1)} %get-tuple-element.136) | copy-start | bytes 196612
  104.9 20.7 %copy-start.18 = (pred[256,256]{1,0:T(8,128)(4,1)S(1)}, pred[256,256]{1,0:T(8,128)(4,1)}, u32[]{:S(2)}) copy-start(pred[256,256]{1,0:T(8,128)(4,1)} %get-tuple-element.133) | copy-start | bytes 196612
  104.9 20.7 %copy-start.19 = (pred[256,256]{1,0:T(8,128)(4,1)S(1)}, pred[256,256]{1,0:T(8,128)(4,1)}, u32[]{:S(2)}) copy-start(pred[256,256]{1,0:T(8,128)(4,1)} %get-tuple-element.134) | copy-start | bytes 196612
  105.0 216.6 %all-gather.21.cloned.1.call-start = ((), (), s32[]{:S(2)}) async-start(), calls=%async_computation.5 | async-start | bytes 18874368 | tf_op jit(solution)/shard_map/all_gather | solution.py:341
  105.2 20.5 %copy-start.20 = (pred[256,256]{1,0:T(8,128)(4,1)S(1)}, pred[256,256]{1,0:T(8,128)(4,1)}, u32[]{:S(2)}) copy-start(pred[256,256]{1,0:T(8,128)(4,1)} %get-tuple-element.131) | copy-start | bytes 196612
  105.2 20.5 %copy-start.21 = (pred[256,256]{1,0:T(8,128)(4,1)S(1)}, pred[256,256]{1,0:T(8,128)(4,1)}, u32[]{:S(2)}) copy-start(pred[256,256]{1,0:T(8,128)(4,1)} %get-tuple-element.132) | copy-start | bytes 196612
  105.2 20.5 %copy-start.22 = (pred[256,256]{1,0:T(8,128)(4,1)S(1)}, pred[256,256]{1,0:T(8,128)(4,1)}, u32[]{:S(2)}) copy-start(pred[256,256]{1,0:T(8,128)(4,1)} %get-tuple-element.129) | copy-start | bytes 196612
  105.2 20.5 %copy-start.23 = (pred[256,256]{1,0:T(8,128)(4,1)S(1)}, pred[256,256]{1,0:T(8,128)(4,1)}, u32[]{:S(2)}) copy-start(pred[256,256]{1,0:T(8,128)(4,1)} %get-tuple-element.130) | copy-start | bytes 196612
  105.2 20.5 %copy-start.24 = (pred[256,256]{1,0:T(8,128)(4,1)S(1)}, pred[256,256]{1,0:T(8,128)(4,1)}, u32[]{:S(2)}) copy-start(pred[256,256]{1,0:T(8,128)(4,1)} %get-tuple-element.127) | copy-start | bytes 196612
  105.2 20.5 %copy-start.25 = (pred[256,256]{1,0:T(8,128)(4,1)S(1)}, pred[256,256]{1,0:T(8,128)(4,1)}, u32[]{:S(2)}) copy-start(pred[256,256]{1,0:T(8,128)(4,1)} %get-tuple-element.128) | copy-start | bytes 196612
  105.2 20.5 %copy-start.26 = (pred[256,256]{1,0:T(8,128)(4,1)S(1)}, pred[256,256]{1,0:T(8,128)(4,1)}, u32[]{:S(2)}) copy-start(pred[256,256]{1,0:T(8,128)(4,1)} %get-tuple-element.125) | copy-start | bytes 196612
  105.2 20.5 %copy-start.27 = (pred[256,256]{1,0:T(8,128)(4,1)S(1)}, pred[256,256]{1,0:T(8,128)(4,1)}, u32[]{:S(2)}) copy-start(pred[256,256]{1,0:T(8,128)(4,1)} %get-tuple-element.126) | copy-start | bytes 196612
  105.3 20.5 %copy-start.28 = (pred[256,256]{1,0:T(8,128)(4,1)S(1)}, pred[256,256]{1,0:T(8,128)(4,1)}, u32[]{:S(2)}) copy-start(pred[256,256]{1,0:T(8,128)(4,1)} %get-tuple-element.123) | copy-start | bytes 196612
  105.3 20.5 %copy-start.29 = (pred[256,256]{1,0:T(8,128)(4,1)S(1)}, pred[256,256]{1,0:T(8,128)(4,1)}, u32[]{:S(2)}) copy-start(pred[256,256]{1,0:T(8,128)(4,1)} %get-tuple-element.124) | copy-start | bytes 196612
  105.3 20.5 %copy-start.30 = (pred[256,256]{1,0:T(8,128)(4,1)S(1)}, pred[256,256]{1,0:T(8,128)(4,1)}, u32[]{:S(2)}) copy-start(pred[256,256]{1,0:T(8,128)(4,1)} %get-tuple-element.121) | copy-start | bytes 196612
  105.3 20.5 %copy-start.31 = (pred[256,256]{1,0:T(8,128)(4,1)S(1)}, pred[256,256]{1,0:T(8,128)(4,1)}, u32[]{:S(2)}) copy-start(pred[256,256]{1,0:T(8,128)(4,1)} %get-tuple-element.122) | copy-start | bytes 196612
  105.3 20.5 %copy-start.36 = (f32[16]{0:T(128)S(1)}, f32[16]{0:T(128)}, u32[]{:S(2)}) copy-start(f32[16]{0:T(128)} %get-tuple-element.82) | copy-start | bytes 196
  105.3 20.5 %copy-start.37 = (f32[16]{0:T(128)S(1)}, f32[16]{0:T(128)}, u32[]{:S(2)}) copy-start(f32[16]{0:T(128)} %get-tuple-element.83) | copy-start | bytes 196
  105.3 20.5 %copy-start.38 = (f32[16]{0:T(128)S(1)}, f32[16]{0:T(128)}, u32[]{:S(2)}) copy-start(f32[16]{0:T(128)} %get-tuple-element.84) | copy-start | bytes 196
  105.3 20.5 %copy-start.39 = (f32[16]{0:T(128)S(1)}, f32[16]{0:T(128)}, u32[]{:S(2)}) copy-start(f32[16]{0:T(128)} %get-tuple-element.85) | copy-start | bytes 196
  105.3 20.5 %copy-start.40 = (f32[16]{0:T(128)S(1)}, f32[16]{0:T(128)}, u32[]{:S(2)}) copy-start(f32[16]{0:T(128)} %get-tuple-element.86) | copy-start | bytes 196
  199.8 36.9 %copy-start.32 = (s32[8,128,2]{1,2,0:T(2,128)S(1)}, s32[8,128,2]{1,2,0:T(2,128)}, u32[]{:S(2)}) copy-start(s32[8,128,2]{1,2,0:T(2,128)} %param.29) | copy-start | bytes 24580
  240.7 111.2 %copy-start.4 = (s32[1024,2]{1,0:T(8,128)}, s32[1024,2]{1,0:T(8,128)S(1)}, u32[]{:S(2)}) copy-start(s32[1024,2]{1,0:T(8,128)S(1)} %add_select_fusion.slot_ref) | copy-start | bytes 24580
  351.9 211.9 %all-to-all-start = ((bf16[8,512,1024]{2,1,0:T(8,128)(2,1)}), bf16[8,512,1024]{2,1,0:T(8,128)(2,1)}, u32[]{:S(2)}, u32[]{:S(2)}) async-start(bf16[8,512,1024]{2,1,0:T(8,128)(2,1)} %experts.1), calls=%async_computation | async-start | bytes 16777216 | tf_op jit(solution)/shard_map/all_to_all | solution.py:345
  355.9 173.9 %collective-permute-start.6 = (bf16[4,256,1024]{2,1,0:T(8,128)(2,1)}, bf16[4,256,1024]{2,1,0:T(8,128)(2,1)}, u32[]{:S(2)}, u32[]{:S(2)}) collective-permute-start(bf16[4,256,1024]{2,1,0:T(8,128)(2,1)} %bitcast.50), channel_id=1, source_target_pairs={{0,4},{4,0},{1,5},{5,1},{2,6},{6,2},{3,7},{7,3}} | collective-permute-start | bytes 6291464 | tf_op jit(solution)/shard_map/ppermute | solution.py:293
  357.9 158.2 %collective-permute-start.7 = (bf16[4,128,1024]{2,1,0:T(8,128)(2,1)S(1)}, bf16[4,128,1024]{2,1,0:T(8,128)(2,1)S(1)}, u32[]{:S(2)}, u32[]{:S(2)}) collective-permute-start(bf16[4,128,1024]{2,1,0:T(8,128)(2,1)S(1)} %get-tuple-element.103), channel_id=1, source_target_pairs={{0,4},{4,0},{1,5},{5,1},{2,6},{6,2},{3,7},{7,3}} | collective-permute-start | bytes 3145736 | tf_op jit(solution)/shard_map/ppermute | solution.py:293
  (17 other events, 220.3 us)
Sparse Core Ops, SparseCore 0:
  30.2 23.6 all-gather.14
  55.4 26.0 all-gather.12
  90.2 13.7 all-gather.18
  105.3 25.4 all-gather.16
  236.8 84.7 all-gather.20

commit v2 on v1

--- a/solution.py
+++ b/solution.py
@@ -137,127 +137,247 @@
     )(rows, ln, *weights)
 
 
-def cache_body(tp_ref, mine_ref, theirs_ref, ln_ref, wk_ref, wv_ref, *rest):
-    k_ref, v_ref = rest[-2:]
-    step = pl.program_id(0)
-    x = jnp.where(step < pl.num_programs(0) // 2, mine_ref[0], theirs_ref[0])
-    a = rms_rows(x, ln_ref[0])
-    for w_ref, out_ref in ((wk_ref, k_ref), (wv_ref, v_ref)):
-        full = mm(a, w_ref[0]).astype(BF16)
-        for head in range(out_ref.shape[2]):
-            out_ref[0, 0, head] = full[:, head * 64:(head + 1) * 64]
-
-
-def cache_layer(layer, tp, mine, theirs, ln, w_key, w_value, caches=None):
-    half, seq_len, d_model = mine.shape
+def axis_neighbours(tp, ep):
+    core = lax.rem(ep, 2)
+    beside = ep + 1 - 2 * core
+    return beside, lax.rem(ep + 2, 4), lax.rem(beside + 2, 4)
+
+
+def remote(src, dst, send, recv, tp, ep):
+    return pltpu.make_async_remote_copy(
+        src_ref=src, dst_ref=dst, send_sem=send, recv_sem=recv,
+        device_id=(lax.axis_index('dp'), tp, ep), device_id_type=pl.DeviceIdType.MESH)
+
+
+def moe_body(h2_ref, h1_ref, x0_ref, x0t_ref, slot_row_ref, slot_col_ref, ids_ref, ln_ref, ln_attn_ref, router_ref,
+             w_in_hbm, w_out_hbm, wk_hbm, wv_hbm,
+             out_ref, k_ref, v_ref, h1t_ref,
+             hall, res, ret, w_in, w_out, wkv, acc, slots_all, gates, xbuf, kvbuf,
+             in_sem, cache_sem, store_sem, slot_send, slot_recv, hs_send, hs_recv, ret_send, ret_recv, h1_send, h1_recv):
+    tp, ep = lax.axis_index('tp'), lax.axis_index('ep')
+    other = 1 - tp
+    ep1, ep2, ep3 = axis_neighbours(tp, ep)
+    me = tp * 4 + ep
+    seqs, seq_len, d_model = h2_ref.shape
+    tokens = acc.shape[0]
+    rows = res.shape[1]
+    half_pos = seq_len // 2
+    experts = w_in.shape[0]
+    capacity = rows // experts
+
+    loads = [pltpu.make_async_copy(a, b, in_sem.at[n]) for n, (a, b) in enumerate((
+        (x0_ref, xbuf), (wk_hbm, wkv.at[0]), (wv_hbm, wkv.at[1]), (h2_ref, hall.at[me]),
+        (w_in_hbm, w_in), (w_out_hbm, w_out)))]
+    for load in loads:
+        load.start()
+    slots_all[me] = slot_row_ref[...]
+
+    barrier = pltpu.get_barrier_semaphore()
+    peers = [(other, ep), (tp, ep2), (tp, ep1), (other, ep1), (other, ep2), (tp, ep3), (other, ep3)]
+    for peer_tp, peer_ep in peers:
+        pl.semaphore_signal(barrier, inc=1, device_id=(lax.axis_index('dp'), peer_tp, peer_ep), device_id_type=pl.DeviceIdType.MESH)
+    pl.semaphore_wait(barrier, len(peers))
+
+    def block(owner):
+        return hall.at[owner]
+
+    send_y = remote(h2_ref, block(me), hs_send.at[0], hs_recv.at[me], other, ep)
+    send_x = remote(h2_ref, block(me), hs_send.at[1], hs_recv.at[me], tp, ep2)
+    send_c = remote(h2_ref, block(me), hs_send.at[2], hs_recv.at[me], tp, ep1)
+    for copy in (send_y, send_x, send_c):
+        copy.start()
+    slot_copies = [remote(slot_row_ref, slots_all.at[me], slot_send.at[n], slot_recv.at[me], *peer) for n, peer in enumerate(peers)]
+    for copy in slot_copies:
+        copy.start()
+    send_h1 = remote(h1_ref, h1t_ref, h1_send, h1_recv, other, ep)
+    send_h1.start()
+
+    def arrived(ref, sem):
+        remote(ref, ref, hs_send.at[0], sem, tp, ep).wait_recv()
+
+    def block_arrived(owner):
+        arrived(hall.at[owner], hs_recv.at[owner])
+
+    def cache_part(source, layer, owner, load=None):
+        if load is None:
+            load = pltpu.make_async_copy(source, xbuf, cache_sem)
+            load.start()
+        load.wait()
+
+        @pl.loop(0, seqs)
+        def _(s):
+            a = rms_rows(xbuf[s], ln_attn_ref[layer])
+            for n, ref in enumerate((k_ref, v_ref)):
+                full = mm(a, wkv[n, layer])
+                kvbuf[s, n] = full.T.astype(BF16).reshape(kvbuf.shape[2:])
+                pltpu.make_async_copy(kvbuf.at[s, n], ref.at[layer, owner * seqs + s], store_sem.at[s, n]).start()
+
+        @pl.loop(0, seqs)
+        def _(s):
+            for n, ref in enumerate((k_ref, v_ref)):
+                pltpu.make_async_copy(kvbuf.at[s, n], ref.at[layer, owner * seqs + s], store_sem.at[s, n]).wait()
+
+    loads[1].wait()
+    loads[2].wait()
+    cache_part(x0_ref, 0, tp, loads[0])
+    cache_part(x0t_ref, 0, other)
+    cache_part(h1_ref, 1, tp)
+
+    y_owner, x_owner, c_owner = other * 4 + ep, tp * 4 + ep2, tp * 4 + ep1
+    yx_owner, yc_owner, xc_owner, yxc_owner = other * 4 + ep2, other * 4 + ep1, tp * 4 + ep3, other * 4 + ep3
+    block_arrived(y_owner)
+    fwd_yx = remote(block(y_owner), block(y_owner), hs_send.at[3], hs_recv.at[y_owner], tp, ep2)
+    fwd_yc = remote(block(y_owner), block(y_owner), hs_send.at[4], hs_recv.at[y_owner], tp, ep1)
+    fwd_yx.start()
+    fwd_yc.start()
+    loads[3].wait()
+
+    def own_tokens(owner):
+        return hall[owner, :, pl.ds(pl.multiple_of(tp * half_pos, half_pos), half_pos), :].reshape(tokens // 2, d_model)
+
+    for part in range(2):
+        at = slice(part * (tokens // 2), (part + 1) * (tokens // 2))
+        h_own = own_tokens(part * 4 + ep)
+        acc[at] = h_own.astype(F32)
+        b = rms_rows(h_own, ln_ref[0])
+        logits = jnp.dot(b.astype(F32), router_ref[...], precision=lax.Precision.HIGHEST, preferred_element_type=F32)
+        grown = jnp.exp(logits - jnp.max(logits, axis=-1, keepdims=True))
+        probs = grown / jnp.sum(grown, axis=-1, keepdims=True)
+        lanes = lax.broadcasted_iota(jnp.int32, probs.shape, 1)
+        picked = [jnp.sum(jnp.where(ids_ref[at, c:c + 1] == lanes, probs, 0.0), axis=-1, keepdims=True) for c in range(2)]
+        both = picked[0] + picked[1]
+        gates[at, 0:1] = picked[0] / both
+        gates[at, 1:2] = picked[1] / both
+
+    block_arrived(x_owner)
+    fwd_xc = remote(block(x_owner), block(x_owner), hs_send.at[5], hs_recv.at[x_owner], tp, ep1)
+    fwd_xc.start()
+    for peer_tp, peer_ep in peers:
+        arrived(slots_all.at[peer_tp * 4 + peer_ep], slot_recv.at[peer_tp * 4 + peer_ep])
+    loads[4].wait()
+    loads[5].wait()
+
+    def run_group(i, k):
+        dest = k * 4 + i
+        slots = slots_all[dest]
+        want = me * rows + lax.broadcasted_iota(jnp.int32, (rows, tokens // 2), 0)
+        chosen = None
+        for part in range(2):
+            h = hall[part * 4 + i, :, pl.ds(pl.multiple_of(k * half_pos, half_pos), half_pos), :].reshape(tokens // 2, d_model)
+            at = slice(part * (tokens // 2), (part + 1) * (tokens // 2))
+            pick = jnp.logical_or(slots[0:1, at] == want, slots[1:2, at] == want)
+            term = mm(jnp.where(pick, 1.0, 0.0).astype(BF16), h)
+            chosen = term if chosen is None else chosen + term
+        b = rms_rows(chosen, ln_ref[0])
+        for e in range(experts):
+            at = slice(e * capacity, (e + 1) * capacity)
+            hid = jax.nn.gelu(mm(b[at], w_in[e])).astype(BF16)
+            res[dest, at] = mm(hid, w_out[e]).astype(BF16)
+        return dest
+
+    def give_back(i, k):
+        dest = k * 4 + i
+        return remote(res.at[dest], ret.at[me], ret_send.at[dest], ret_recv.at[me], k, i)
+
+    def add_rows(source_ref, owner):
+        step = 256
+
+        @pl.loop(0, tokens // step)
+        def _(r):
+            at = pl.ds(pl.multiple_of(r * step, step), step)
+            columns = owner * rows + lax.broadcasted_iota(jnp.int32, (step, rows), 1)
+            total = acc[at, :]
+            for c in range(2):
+                pick = jnp.where(slot_col_ref[at, c:c + 1] == columns, 1.0, 0.0).astype(BF16)
+                total = total + gates[at, c:c + 1] * mm(pick, source_ref[...])
+            acc[at, :] = total
+
+    block_arrived(c_owner)
+    block_arrived(yc_owner)
+
+    @pl.loop(0, 4)
+    def _(t):
+        late = t // 2
+        beside = lax.rem((t + 1) // 2, 2)
+        i = ep + beside * (ep1 - ep)
+        k = late * tp + (1 - late) * other
+        run_group(i, k)
+
+        @pl.when(t < 3)
+        def _():
+            give_back(i, k).start()
+
+    add_rows(res.at[me], me)
+
+    block_arrived(yx_owner)
+    fwd_yxc = remote(block(yx_owner), block(yx_owner), hs_send.at[6], hs_recv.at[yx_owner], tp, ep1)
+    fwd_yxc.start()
+
+    def far_groups(i):
+        @pl.loop(0, 2)
+        def _(t):
+            k = t * tp + (1 - t) * other
+            run_group(i, k)
+            give_back(i, k).start()
+
+    far_groups(ep2)
+    block_arrived(xc_owner)
+    block_arrived(yxc_owner)
+    far_groups(ep3)
+
+    arrived(h1t_ref, h1_recv)
+    cache_part(h1t_ref, 1, other)
+
+    for peer_tp, peer_ep in ((tp, ep1), (other, ep), (other, ep1), (other, ep2), (tp, ep2), (other, ep3), (tp, ep3)):
+        owner = peer_tp * 4 + peer_ep
+        arrived(ret.at[owner], ret_recv.at[owner])
+        add_rows(ret.at[owner], owner)
+    out_ref[...] = acc[...].astype(BF16)
+
+    for copy in (send_y, send_x, send_c, fwd_yx, fwd_yc, fwd_xc, fwd_yxc, send_h1):
+        copy.wait_send()
+    for copy in slot_copies:
+        copy.wait_send()
+    for peer_tp, peer_ep in peers:
+        give_back(peer_ep, peer_tp).wait_send()
+
+
+def moe_layer(h2, h1, x0, x0t, slots, choices, ln, ln_attn, w_router, expert_in, expert_out, w_key, w_value):
+    seqs, seq_len, d_model = h2.shape
+    tokens = seqs * seq_len
+    experts, _, d_ff = expert_in.shape
+    groups = 8
+    rows = experts * 4 * tokens // (experts * groups)
     inner = w_key.shape[2]
     heads = inner // 64
-    shape = jax.ShapeDtypeStruct((2, 2 * half, heads, seq_len, 64), BF16)
-
-    def out_index(t, tp_ref):
-        owner = jnp.where(t < half, tp_ref[0], 1 - tp_ref[0])
-        return layer, owner * half + lax.rem(t, half), 0, 0, 0
-
-    out_spec = pl.BlockSpec((1, 1, heads, seq_len, 64), out_index)
-    own = fixed((1, d_model, inner), (layer, 0, 0))
-    in_specs = [
-        pl.BlockSpec((1, seq_len, d_model), lambda t, tp_ref: (jnp.minimum(t, half - 1), 0, 0)),
-        pl.BlockSpec((1, seq_len, d_model), lambda t, tp_ref: (jnp.maximum(t - half, 0), 0, 0)),
-        fixed((1, d_model), (0, 0)), own, own,
-    ]
-    args = [tp, mine, theirs, ln, w_key, w_value]
-    aliases = {}
-    if caches is not None:
-        in_specs += [pl.BlockSpec(memory_space=pl.ANY)] * 2
-        args += list(caches)
-        aliases = {6: 0, 7: 1}
+    any_spec = pl.BlockSpec(memory_space=pl.ANY)
+    vmem_spec = pl.BlockSpec(memory_space=pltpu.VMEM)
+    cache_shape = jax.ShapeDtypeStruct((2, 2 * seqs, heads, 64, seq_len), BF16)
+    dma = pltpu.SemaphoreType.DMA
     return pl.pallas_call(
-        cache_body,
-        grid_spec=pltpu.PrefetchScalarGridSpec(
-            num_scalar_prefetch=1, grid=(2 * half,), in_specs=in_specs, out_specs=[out_spec, out_spec]),
-        out_shape=[shape, shape],
-        input_output_aliases=aliases,
-        compiler_params=pltpu.CompilerParams(vmem_limit_bytes=VMEM_LIMIT),
-        cost_estimate=pl.CostEstimate(flops=8 * half * seq_len * d_model * inner, bytes_accessed=14 << 20, transcendentals=0),
-        name=f"cache{layer}",
-    )(*args)
-
-
-def experts_body(dev_ref, h_ref, slot_ref, ln_ref, w_in_ref, w_out_ref, out_ref):
-    h = h_ref[...].reshape(-1, h_ref.shape[-1])
-    tokens = h.shape[0]
-    experts = w_in_ref.shape[0]
-    rows = out_ref.shape[1]
-    capacity = rows // experts
-    want = dev_ref[0] * rows + lax.broadcasted_iota(jnp.int32, (rows, tokens), 0)
-    slots = slot_ref[0]
-    pick = jnp.logical_or(slots[0:1] == want, slots[1:2] == want)
-    chosen = mm(jnp.where(pick, 1.0, 0.0).astype(BF16), h)
-    b = rms_rows(chosen, ln_ref[0])
-    for e in range(experts):
-        at = slice(e * capacity, (e + 1) * capacity)
-        hid = jax.nn.gelu(mm(b[at], w_in_ref[e])).astype(BF16)
-        out_ref[0, at] = mm(hid, w_out_ref[e]).astype(BF16)
-
-
-def experts_layer(dev, h_all, slots, ln, expert_in, expert_out):
-    tp_n, ep_n, seqs, _, positions, d_model = h_all.shape
-    experts = expert_in.shape[0]
-    tokens = tp_n * seqs * positions
-    groups = tp_n * ep_n
-    rows = experts * (4 * tokens // (experts * groups))
-    flops = groups * 2 * rows * d_model * (tokens + 2 * expert_in.shape[2])
-    return pl.pallas_call(
-        experts_body,
-        grid_spec=pltpu.PrefetchScalarGridSpec(
-            num_scalar_prefetch=1,
-            grid=(groups,),
-            in_specs=[
-                pl.BlockSpec((tp_n, 1, seqs, 1, positions, d_model), lambda g, d: (0, g % ep_n, 0, g // ep_n, 0, 0)),
-                pl.BlockSpec((1, 2, tokens), lambda g, d: (g, 0, 0)),
-                fixed((1, d_model), (0, 0)),
-                fixed(expert_in.shape, (0, 0, 0)),
-                fixed(expert_out.shape, (0, 0, 0)),
-            ],
-            out_specs=pl.BlockSpec((1, rows, d_model), lambda g, d: (g, 0, 0)),
-        ),
-        out_shape=jax.ShapeDtypeStruct((groups, rows, d_model), BF16),
-        compiler_params=pltpu.CompilerParams(vmem_limit_bytes=VMEM_LIMIT),
-        cost_estimate=pl.CostEstimate(flops=flops, bytes_accessed=32 << 20, transcendentals=0),
-        name="experts",
-    )(dev, h_all, slots, ln, expert_in, expert_out)
-
-
-def combine_body(h_ref, slot_ref, gate_ref, rows_ref, out_ref):
-    block = h_ref.shape[0]
-    total = rows_ref.shape[0]
-    columns = lax.broadcasted_iota(jnp.int32, (block, total), 1)
-    out = h_ref[...].astype(F32)
-    parts = []
-    for c in range(2):
-        pick = jnp.where(slot_ref[:, c:c + 1] == columns, 1.0, 0.0).astype(BF16)
-        parts.append(gate_ref[:, c:c + 1] * mm(pick, rows_ref[...]))
-    out_ref[...] = (out + (parts[0] + parts[1])).astype(BF16)
-
-
-def combine_layer(h, slots, gates, rows, block=128):
-    n, d_model = h.shape
-    total = rows.shape[0]
-    return pl.pallas_call(
-        combine_body,
-        grid=(n // block,),
-        in_specs=[
-            pl.BlockSpec((block, d_model), lambda i: (i, 0)),
-            pl.BlockSpec((block, 2), lambda i: (i, 0)),
-            pl.BlockSpec((block, 2), lambda i: (i, 0)),
-            fixed(rows.shape, (0, 0)),
+        moe_body,
+        in_specs=[any_spec] * 4 + [vmem_spec] * 6 + [any_spec] * 4,
+        out_specs=[vmem_spec, any_spec, any_spec, any_spec],
+        out_shape=[jax.ShapeDtypeStruct((tokens, d_model), BF16), cache_shape, cache_shape, jax.ShapeDtypeStruct(h1.shape, BF16)],
+        scratch_shapes=[
+            pltpu.VMEM((groups,) + h2.shape, BF16),
+            pltpu.VMEM((groups, rows, d_model), BF16),
+            pltpu.VMEM((groups, rows, d_model), BF16),
+            pltpu.VMEM(expert_in.shape, BF16),
+            pltpu.VMEM(expert_out.shape, BF16),
+            pltpu.VMEM((2, 2, d_model, inner), BF16),
+            pltpu.VMEM((tokens, d_model), F32),
+            pltpu.VMEM((groups, 2, tokens), jnp.int32),
+            pltpu.VMEM((tokens, 2), F32),
+            pltpu.VMEM(h1.shape, BF16),
+            pltpu.VMEM((seqs, 2, heads, 64, seq_len), BF16),
+            dma((6,)), dma, dma((seqs, 2)), dma((7,)), dma((groups,)), dma((7,)), dma((groups,)),
+            dma((groups,)), dma((groups,)), dma, dma,
         ],
-        out_specs=pl.BlockSpec((block, d_model), lambda i: (i, 0)),
-        out_shape=jax.ShapeDtypeStruct(h.shape, BF16),
-        compiler_params=pltpu.CompilerParams(vmem_limit_bytes=VMEM_LIMIT),
-        cost_estimate=pl.CostEstimate(flops=4 * n * total * d_model, bytes_accessed=13 << 20, transcendentals=0),
-        name="combine",
-    )(h, slots, gates, rows)
+        compiler_params=pltpu.CompilerParams(vmem_limit_bytes=67043328, collective_id=2, has_side_effects=True),
+        cost_estimate=pl.CostEstimate(flops=40_000_000_000, bytes_accessed=64 << 20, transcendentals=0),
+        name="moe",
+    )(h2, h1, x0, x0t, slots.T, slots, choices, ln, ln_attn, w_router, expert_in, expert_out, w_key, w_value)
 
 
 def slot_table(choices, num_experts, capacity):
@@ -327,31 +447,14 @@
         capacity = 4 * tokens // num_experts
         choices = expert_ids.reshape(tokens, 2)
         slots = slot_table(choices, num_experts, capacity)
-        slots_all = lax.all_gather(slots.T, ('tp', 'ep'), axis=0, tiled=False)
 
         h = attention_layer(0, x0, ln_attn[0:1], w_query, w_key, w_value, wqkv0, w_out, wo0, bias_map(bias_all[0], tp_n * positions))
         h1 = ffn_layer(h.reshape(tokens, d_model), ln_ffn[0:1], w_gate, w_up, w_down, gu_other, wd_other).reshape(h.shape)
         h2 = attention_layer(1, h1, ln_attn[1:2], w_query, w_key, w_value, wqkv1, w_out, wo1, bias_map(bias_all[1], tp_n * positions))
 
-        tp_arr = tp.reshape(1).astype(jnp.int32)
         x0_theirs = whole_seq(given, swap(kept))
-        caches = cache_layer(0, tp_arr, x0, x0_theirs, ln_attn[0:1], w_key, w_value)
-        k_cache, v_cache = cache_layer(1, tp_arr, h1, swap(h1), ln_attn[1:2], w_key, w_value, caches)
-
-        h_all = lax.all_gather(h2, ('tp', 'ep'), axis=0, tiled=False)
-        h_all = h_all.reshape(tp_n, ep_n, half, tp_n, positions, d_model)
-        dev = (tp * ep_n + ep).reshape(1).astype(jnp.int32)
-        results = experts_layer(dev, h_all, slots_all, ln_ffn[1:2], expert_in, expert_out)
-        returned = lax.all_to_all(results, ('tp', 'ep'), 0, 0, tiled=True).reshape(num_experts * capacity, d_model)
-
-        h_own = lax.dynamic_slice(h_all, (0, ep, 0, tp, 0, 0), (tp_n, 1, half, 1, positions, d_model)).reshape(tokens, d_model)
-        b = rms_rows(h_own, ln_ffn[1])
-        logits = jnp.dot(b.astype(F32), w_router, precision=lax.Precision.HIGHEST)
-        probs = jax.nn.softmax(logits, axis=-1)
-        hot = choices[:, :, None] == jnp.arange(num_experts, dtype=jnp.int32)
-        picked = jnp.sum(jnp.where(hot, probs[:, None, :], 0.0), axis=-1)
-        gates = picked / jnp.sum(picked, axis=-1, keepdims=True)
-        hidden = combine_layer(h_own, slots, gates, returned).reshape(hidden_in.shape)
-        return hidden, k_cache, v_cache
+        hidden, k_cache, v_cache, _ = moe_layer(
+            h2, h1, x0, x0_theirs, slots, choices, ln_ffn[1:2], ln_attn, w_router, expert_in, expert_out, w_key, w_value)
+        return hidden.reshape(hidden_in.shape), jnp.swapaxes(k_cache, 3, 4), jnp.swapaxes(v_cache, 3, 4)
 
     return jax.shard_map(device_fn, mesh=mesh, in_specs=in_specs, out_specs=(act_spec, cache_spec, cache_spec), check_vma=False)

time: 601 us -> 482 us (0.80)
  waiting for transfers between devices: 280 us -> 58.1 us
  Pallas kernels: 158 us -> 284 us
  blocking collectives: 11.8 us -> 0 us
    ppermute x8 -> x7, waiting for transfers between devices: 211 us -> 58.1 us  [device_fn(): swap = lambda value: lax.ppermute(value, 'tp', TP_SWAP)]
    pallas_call x4 -> x1, Pallas kernels: 76.9 us -> 203 us  [moe_layer(): pl.pallas_call(moe_body, in_specs=[any_spec] * 4 + [vmem_spec] * 6 + [any...]
    all_gather x1 -> x0, waiting for transfers between devices: 68.8 us -> none  [device_fn(): h_all = lax.all_gather(h2, ('tp', 'ep'), axis=0, tiled=False)]
    all_gather x1 -> x0, blocking collectives: 11.8 us -> none  [device_fn(): slots_all = lax.all_gather(slots.T, ('tp', 'ep'), axis=0, tiled=False)]
    unnamed x107 -> x80, local copies, waits for them, and re-layouts: 21 us -> 15.2 us
  transfers between devices with their start and end apart: 14 -> 11, of which waited for: 6 -> 3; matrix products, arithmetic and copies ran while one was open for 18% -> 19% of each run, Pallas kernels for 11% -> 9%
where the time goes in v2:
time: 482 us; the launch traced here: 475 us
  Pallas kernels  284 us (59%)
  other arithmetic  63.4 us (13%)
  waiting for transfers between devices  58.1 us (12%)
  local copies, waits for them, and re-layouts  43.7 us (9%)
  between operations  14.9 us (3%)
  starting transfers between devices  11.1 us (2%)
    pallas_call x1, Pallas kernels, moe_layer(): pl.pallas_call(moe_body, in_specs=[any_spec] * 4 + [vmem_spec] * 6 + [any...  203 us
    pallas_call x2, Pallas kernels, attention_layer(): pl.pallas_call(attention_body, grid=(seqs,), in_specs=[pl.BlockSpec((1, s...  73.3 us
    ppermute x7, waiting for transfers between devices, device_fn(): swap = lambda value: lax.ppermute(value, 'tp', TP_SWAP)  58.1 us
    select_n x2, other arithmetic, bias_map(): return jnp.where(rel[None] >= 0, out, -jnp.inf)  39.5 us
    unnamed x80, local copies, waits for them, and re-layouts  15.2 us
    eq x15, other arithmetic, bias_map(): out = jnp.where(bucket[None] == k, table[:, k][:, None, None], out)  12.2 us
    ppermute x7, starting transfers between devices, device_fn(): swap = lambda value: lax.ppermute(value, 'tp', TP_SWAP)  10.7 us
  transfers between devices with their start and end apart: 11, of which 3 were waited for; matrix products, arithmetic and copies ran while one was open for 19% of the time, Pallas kernels for 9%

profile of v2, /device:TPU:0, one launch (start us, length us, event | category | flops | bytes accessed | tf_op | source)
XLA Modules:
  0.0 475.5 jit_solution(1070846362093328814)
XLA Ops:
  7.2 1.1 constant_dynamic-slice_fusion
  9.2 2.7 fusion.21
  11.9 0.9 constant_dynamic-slice_fusion.2
  12.8 1.0 pad_maximum_fusion.2
  13.8 3.4 collective-permute-start.2
  17.2 14.7 %collective-permute-done.2 = bf16[320,1024]{1,0:T(8,128)(2,1)S(1)} collective-permute-done((bf16[320,1024]{1,0:T(8,128)(2,1)S(1)}, bf16[320,1024]{1,0:T(8,128)(2,1)S(1)}, u32[]{:S(2)}, u32[]{:S(2)}) %collective-permute-start.2) | collective-permute-done | bytes 655392 | tf_op jit(solution)/shard_map/ppermute | solution.py:413
  32.9 1.1 fusion.22
  34.9 1.1 fusion.23
  36.0 1.1 fusion.24
  37.2 1.8 collective-permute-start.1
  38.9 17.0 %collective-permute-done.1 = bf16[256,1536]{1,0:T(8,128)(2,1)S(1)} collective-permute-done((bf16[256,1536]{1,0:T(8,128)(2,1)S(1)}, bf16[256,1536]{1,0:T(8,128)(2,1)S(1)}, u32[]{:S(2)}, u32[]{:S(2)}) %collective-permute-start.1) | collective-permute-done | bytes 786464 | tf_op jit(solution)/shard_map/ppermute | solution.py:413
  56.9 1.5 collective-permute-start.3
  58.4 1.8 constant_dynamic-slice_fusion.4
  60.8 1.0 dynamic-slice_bitcast_fusion.3
  61.7 1.1 dynamic-slice_bitcast_fusion.1
  62.8 0.9 pad_maximum_fusion.1
  63.7 1.5 collective-permute-start.4
  65.2 1.0 dynamic-slice_bitcast_fusion
  66.8 1.5 collective-permute-start.6
  72.3 0.9 broadcast_compare_fusion.9
  74.1 0.9 broadcast_compare_fusion.13
  75.0 0.9 broadcast_compare_fusion.15
  78.6 1.0 copy.31
  80.5 0.9 broadcast_compare_fusion.23
  81.4 0.9 broadcast_compare_fusion.25
  82.3 26.4 %collective-permute-done.5 = bf16[128,1024]{1,0:T(8,128)(2,1)S(1)} collective-permute-done((bf16[128,1024]{1,0:T(8,128)(2,1)S(1)}, bf16[128,1024]{1,0:T(8,128)(2,1)S(1)}, u32[]{:S(2)}, u32[]{:S(2)}) %collective-permute-start.5) | collective-permute-done | bytes 262176 | tf_op jit(solution)/shard_map/ppermute | solution.py:413
  109.7 0.9 broadcast_compare_fusion.27
  110.6 1.4 fusion.26
  111.9 1.4 fusion.25
  113.3 1.2 add_select_fusion.slot_col_ref
  114.5 0.9 broadcast_compare_fusion.29
  116.9 1.9 copy.34.router_ref
  120.1 1.1 slice_reduce_fusion.63
  121.4 20.2 %select_select_fusion.1.bias_ref = f32[16,256,256]{2,1,0:T(8,128)} fusion(f32[16]{0:T(128)S(1)} %get-tuple-element.44, f32[16]{0:T(128)S(1)} %get-tuple-element.45, f32[16]{0:T(128)S(1)} %get-tuple-element.46, f32[16]{0:T(128)S(1)} %get-tuple-element.47, f32[16]{0:T(128)} %get-tuple-element.48, f32[16]{0:T(128)} %get-tuple-element.49, ...), kind=kLoop, calls=%fused_computation.2 | loop fusion | flops 33554432 | bytes 6293504 | tf_op jit(solution)/shard_map/jit(_where)/select_n | solution.py:46
  142.8 19.3 %select_select_fusion.bias_ref = f32[16,256,256]{2,1,0:T(8,128)} fusion(f32[16]{0:T(128)S(1)} %get-tuple-element.12, f32[16]{0:T(128)S(1)} %get-tuple-element.13, f32[16]{0:T(128)S(1)} %get-tuple-element.14, f32[16]{0:T(128)S(1)} %get-tuple-element.15, f32[16]{0:T(128)S(1)} %get-tuple-element.16, f32[16]{0:T(128)S(1)} %get-tuple-element.17, ...), kind=kLoop, calls=%fused_computation.1 | loop fusion | flops 33554432 | bytes 6293504 | tf_op jit(solution)/shard_map/jit(_where)/select_n | solution.py:46
  162.1 4.0 maximum_select_fusion.x_ref.x0_ref
  166.1 3.9 maximum_select_fusion.1.x0t_ref
  170.0 1.9 slice.379
  171.9 2.8 fusion.20
  174.7 1.2 reshape.520.gu_other_ref
  175.8 36.5 %attention0.1 = bf16[4,256,1024]{2,1,0:T(8,128)(2,1)} custom-call(bf16[4,256,1024]{2,1,0:T(8,128)(2,1)} %maximum_select_fusion.x_ref.x0_ref, f32[1,1024]{1,0:T(1,128)} %get-tuple-element.94.ln_ref, bf16[2,1024,512]{2,1,0:T(8,128)(2,1)} %wq_ref.3, bf16[2,1024,512]{2,1,0:T(8,128)(2,1)} %wk_hbm.1, bf16[2,1024,512]{2,1,0:T(8,128)(2,1)} %wv_hbm.1, ...), custom_call_target="tpu_custom_call" | custom-call | flops 9663676416 | bytes 18874368 | tf_op jit(solution)/shard_map/attention0/pallas_call | solution.py:92
  212.3 7.7 %ffn.1 = bf16[1024,1024]{1,0:T(8,128)(2,1)} custom-call(bf16[1024,1024]{1,0:T(8,128)(2,1)} %bitcast.54, f32[1,1024]{1,0:T(1,128)} %get-tuple-element.92.ln_ref, bf16[1024,256]{1,0:T(8,128)(2,1)} %wg_ref.1, bf16[1024,256]{1,0:T(8,128)(2,1)} %wu_ref.1, bf16[256,1024]{1,0:T(8,128)(2,1)} %wd_ref.1, bf16[1024,512]{1,0:T(8,128)(2,1)} %reshape.520.gu_other_ref, ...), custom_call_target="tpu_custom_call" | custom-call | flops 3221225472 | bytes 7340032 | tf_op jit(solution)/shard_map/ffn/pallas_call | solution.py:128
  220.0 36.8 %attention1.1.h2_ref = bf16[4,256,1024]{2,1,0:T(8,128)(2,1)} custom-call(bf16[4,256,1024]{2,1,0:T(8,128)(2,1)} %bitcast.52, f32[1,1024]{1,0:T(1,128)} %get-tuple-element.93.ln_ref, bf16[2,1024,512]{2,1,0:T(8,128)(2,1)} %wq_ref.3, bf16[2,1024,512]{2,1,0:T(8,128)(2,1)} %wk_hbm.1, bf16[2,1024,512]{2,1,0:T(8,128)(2,1)} %wv_hbm.1, ...), custom_call_target="tpu_custom_call" | custom-call | flops 9663676416 | bytes 18874368 | tf_op jit(solution)/shard_map/attention1/pallas_call | solution.py:92
  256.8 202.7 %moe.1 = (bf16[1024,1024]{1,0:T(8,128)(2,1)}, bf16[2,8,8,64,256]{4,3,2,1,0:T(8,128)(2,1)}, bf16[2,8,8,64,256]{4,3,2,1,0:T(8,128)(2,1)}, bf16[4,256,1024]{2,1,0:T(8,128)(2,1)}) custom-call(bf16[4,256,1024]{2,1,0:T(8,128)(2,1)} %attention1.1.h2_ref, bf16[4,256,1024]{2,1,0:T(8,128)(2,1)} %bitcast.53, bf16[4,256,1024]{2,1,0:T(8,128)(2,1)} %maximum_select_fusion.x_ref.x0_ref, ...), custom_call_target="tpu_custom_call" | custom-call | flops 40000000000 | bytes 67108864 | tf_op jit(solution)/shard_map/moe/pallas_call | solution.py:357
  459.5 3.2 copy.42
  462.7 2.1 copy.43
  464.9 1.6 copy-done.1
  466.4 2.0 copy.44
  (124 shorter events, 18.1 us)
Async XLA Ops:
  7.2 162.8 %all-gather.11.cloned.1.call-start = ((), (), s32[]{:S(2)}) async-start(), calls=%async_computation.1 | async-start | bytes 3276800 | tf_op jit(solution)/shard_map/all_gather | solution.py:414
  7.2 25.7 %copy-start.3 = (bf16[2,1024,512]{2,1,0:T(8,128)(2,1)S(1)}, bf16[2,1024,512]{2,1,0:T(8,128)(2,1)}, u32[]{:S(2)}) copy-start(bf16[2,1024,512]{2,1,0:T(8,128)(2,1)} %wq_ref.3) | copy-start | bytes 6291460
  13.8 18.1 %collective-permute-start.2 = (bf16[320,1024]{1,0:T(8,128)(2,1)S(1)}, bf16[320,1024]{1,0:T(8,128)(2,1)S(1)}, u32[]{:S(2)}, u32[]{:S(2)}) collective-permute-start(bf16[320,1024]{1,0:T(8,128)(2,1)S(1)} %pad_maximum_fusion.2), channel_id=1, source_target_pairs={{0,4},{4,0},{1,5},{5,1},{2,6},{6,2},{3,7},{7,3}} | collective-permute-start | bytes 1966088 | tf_op jit(solution)/shard_map/ppermute | solution.py:413
  31.9 0.9 copy-start.8
  32.8 143.0 %all-gather.9.cloned.1.call-start = ((), (), s32[]{:S(2)}) async-start(), calls=%async_computation | async-start | bytes 3932160 | tf_op jit(solution)/shard_map/all_gather | solution.py:414
  32.9 2.0 copy-start.4
  32.9 3.1 copy-start.5
  37.2 18.7 %collective-permute-start.1 = (bf16[256,1536]{1,0:T(8,128)(2,1)S(1)}, bf16[256,1536]{1,0:T(8,128)(2,1)S(1)}, u32[]{:S(2)}, u32[]{:S(2)}) collective-permute-start(bf16[256,1536]{1,0:T(8,128)(2,1)S(1)} %pad_maximum_fusion), channel_id=1, source_target_pairs={{0,4},{4,0},{1,5},{5,1},{2,6},{6,2},{3,7},{7,3}} | collective-permute-start | bytes 2359304 | tf_op jit(solution)/shard_map/ppermute | solution.py:413
  55.9 0.9 copy-start.7
  55.9 12.3 %copy-start.36 = (s32[8,128,2]{1,2,0:T(2,128)S(1)}, s32[8,128,2]{1,2,0:T(2,128)}, u32[]{:S(2)}) copy-start(s32[8,128,2]{1,2,0:T(2,128)} %param.29) | copy-start | bytes 24580
  56.8 163.2 %all-gather.15.cloned.1.call-start = ((), (), s32[]{:S(2)}) async-start(), calls=%async_computation.3 | async-start | bytes 1310720 | tf_op jit(solution)/shard_map/all_gather | solution.py:414
  56.9 62.0 %collective-permute-start.3 = (f32[2,8,32]{2,1,0:T(8,128)}, f32[2,8,32]{2,1,0:T(8,128)}, u32[]{:S(2)}, u32[]{:S(2)}) collective-permute-start(f32[2,8,32]{2,1,0:T(8,128)} %param.22), channel_id=1, source_target_pairs={{0,4},{4,0},{1,5},{5,1},{2,6},{6,2},{3,7},{7,3}} | collective-permute-start | bytes 6152 | tf_op jit(solution)/shard_map/ppermute | solution.py:413
  60.2 101.9 %collective-permute-start = (bf16[4,128,1024]{2,1,0:T(8,128)(2,1)S(1)}, bf16[4,128,1024]{2,1,0:T(8,128)(2,1)}, u32[]{:S(2)}, u32[]{:S(2)}) collective-permute-start(bf16[4,128,1024]{2,1,0:T(8,128)(2,1)S(1)} %get-tuple-element.86), channel_id=1, source_target_pairs={{0,4},{4,0},{1,5},{5,1},{2,6},{6,2},{3,7},{7,3}} | collective-permute-start | bytes 3145736 | tf_op jit(solution)/shard_map/ppermute | solution.py:413
  63.7 57.5 %collective-permute-start.4 = (bf16[256,1536]{1,0:T(8,128)(2,1)}, bf16[256,1536]{1,0:T(8,128)(2,1)}, u32[]{:S(2)}, u32[]{:S(2)}) collective-permute-start(bf16[256,1536]{1,0:T(8,128)(2,1)} %pad_maximum_fusion.1), channel_id=1, source_target_pairs={{0,4},{4,0},{1,5},{5,1},{2,6},{6,2},{3,7},{7,3}} | collective-permute-start | bytes 2359304 | tf_op jit(solution)/shard_map/ppermute | solution.py:413
  66.2 42.5 %collective-permute-start.5 = (bf16[128,1024]{1,0:T(8,128)(2,1)S(1)}, bf16[128,1024]{1,0:T(8,128)(2,1)S(1)}, u32[]{:S(2)}, u32[]{:S(2)}) collective-permute-start(bf16[128,1024]{1,0:T(8,128)(2,1)S(1)} %dynamic-slice_bitcast_fusion), channel_id=1, source_target_pairs={{0,4},{4,0},{1,5},{5,1},{2,6},{6,2},{3,7},{7,3}} | collective-permute-start | bytes 786440 | tf_op jit(solution)/shard_map/ppermute | solution.py:413
  66.8 99.3 %collective-permute-start.6 = (bf16[4,128,1024]{2,1,0:T(8,128)(2,1)S(1)}, bf16[4,128,1024]{2,1,0:T(8,128)(2,1)}, u32[]{:S(2)}, u32[]{:S(2)}) collective-permute-start(bf16[4,128,1024]{2,1,0:T(8,128)(2,1)S(1)} %get-tuple-element.85), channel_id=1, source_target_pairs={{0,4},{4,0},{1,5},{5,1},{2,6},{6,2},{3,7},{7,3}} | collective-permute-start | bytes 3145736 | tf_op jit(solution)/shard_map/ppermute | solution.py:413
  68.4 50.4 %copy-start = (s32[8,128,2]{2,1,0:T(8,128)}, s32[8,128,2]{2,1,0:T(8,128)S(1)}, u32[]{:S(2)}) copy-start(s32[8,128,2]{2,1,0:T(8,128)S(1)} %copy.28) | copy-start | bytes 24580
  108.7 0.7 copy-start.35
  109.4 110.6 %all-gather.13.cloned.1.call-start = ((), (), s32[]{:S(2)}) async-start(), calls=%async_computation.2 | async-start | bytes 3932160 | tf_op jit(solution)/shard_map/all_gather | solution.py:414
  114.5 27.1 %copy-start.6 = (s32[1024,2]{1,0:T(8,128)}, s32[1024,2]{1,0:T(8,128)S(1)}, u32[]{:S(2)}) copy-start(s32[1024,2]{1,0:T(8,128)S(1)} %add_select_fusion.slot_col_ref) | copy-start | bytes 24580
  118.9 23.7 %copy-start.9 = (pred[256,256]{1,0:T(8,128)(4,1)S(1)}, pred[256,256]{1,0:T(8,128)(4,1)}, u32[]{:S(2)}) copy-start(pred[256,256]{1,0:T(8,128)(4,1)} %get-tuple-element.107) | copy-start | bytes 196612
  118.9 23.7 %copy-start.10 = (pred[256,256]{1,0:T(8,128)(4,1)S(1)}, pred[256,256]{1,0:T(8,128)(4,1)}, u32[]{:S(2)}) copy-start(pred[256,256]{1,0:T(8,128)(4,1)} %get-tuple-element.108) | copy-start | bytes 196612
  118.9 23.7 %copy-start.11 = (pred[256,256]{1,0:T(8,128)(4,1)S(1)}, pred[256,256]{1,0:T(8,128)(4,1)}, u32[]{:S(2)}) copy-start(pred[256,256]{1,0:T(8,128)(4,1)} %get-tuple-element.109) | copy-start | bytes 196612
  118.9 23.7 %copy-start.12 = (pred[256,256]{1,0:T(8,128)(4,1)S(1)}, pred[256,256]{1,0:T(8,128)(4,1)}, u32[]{:S(2)}) copy-start(pred[256,256]{1,0:T(8,128)(4,1)} %get-tuple-element.110) | copy-start | bytes 196612
  118.9 23.7 %copy-start.13 = (pred[256,256]{1,0:T(8,128)(4,1)S(1)}, pred[256,256]{1,0:T(8,128)(4,1)}, u32[]{:S(2)}) copy-start(pred[256,256]{1,0:T(8,128)(4,1)} %get-tuple-element.111) | copy-start | bytes 196612
  118.9 23.7 %copy-start.14 = (pred[256,256]{1,0:T(8,128)(4,1)S(1)}, pred[256,256]{1,0:T(8,128)(4,1)}, u32[]{:S(2)}) copy-start(pred[256,256]{1,0:T(8,128)(4,1)} %get-tuple-element.112) | copy-start | bytes 196612
  118.9 23.7 %copy-start.15 = (pred[256,256]{1,0:T(8,128)(4,1)S(1)}, pred[256,256]{1,0:T(8,128)(4,1)}, u32[]{:S(2)}) copy-start(pred[256,256]{1,0:T(8,128)(4,1)} %get-tuple-element.113) | copy-start | bytes 196612
  121.2 21.4 %copy-start.16 = (pred[256,256]{1,0:T(8,128)(4,1)S(1)}, pred[256,256]{1,0:T(8,128)(4,1)}, u32[]{:S(2)}) copy-start(pred[256,256]{1,0:T(8,128)(4,1)} %get-tuple-element.114) | copy-start | bytes 196612
  121.2 21.4 %copy-start.17 = (pred[256,256]{1,0:T(8,128)(4,1)S(1)}, pred[256,256]{1,0:T(8,128)(4,1)}, u32[]{:S(2)}) copy-start(pred[256,256]{1,0:T(8,128)(4,1)} %get-tuple-element.115) | copy-start | bytes 196612
  121.3 21.4 %copy-start.18 = (pred[256,256]{1,0:T(8,128)(4,1)S(1)}, pred[256,256]{1,0:T(8,128)(4,1)}, u32[]{:S(2)}) copy-start(pred[256,256]{1,0:T(8,128)(4,1)} %get-tuple-element.116) | copy-start | bytes 196612
  121.3 21.4 %copy-start.19 = (pred[256,256]{1,0:T(8,128)(4,1)S(1)}, pred[256,256]{1,0:T(8,128)(4,1)}, u32[]{:S(2)}) copy-start(pred[256,256]{1,0:T(8,128)(4,1)} %get-tuple-element.117) | copy-start | bytes 196612
  121.3 21.4 %copy-start.20 = (pred[256,256]{1,0:T(8,128)(4,1)S(1)}, pred[256,256]{1,0:T(8,128)(4,1)}, u32[]{:S(2)}) copy-start(pred[256,256]{1,0:T(8,128)(4,1)} %get-tuple-element.118) | copy-start | bytes 196612
  121.3 21.4 %copy-start.21 = (pred[256,256]{1,0:T(8,128)(4,1)S(1)}, pred[256,256]{1,0:T(8,128)(4,1)}, u32[]{:S(2)}) copy-start(pred[256,256]{1,0:T(8,128)(4,1)} %get-tuple-element.119) | copy-start | bytes 196612
  121.3 21.4 %copy-start.22 = (pred[256,256]{1,0:T(8,128)(4,1)S(1)}, pred[256,256]{1,0:T(8,128)(4,1)}, u32[]{:S(2)}) copy-start(pred[256,256]{1,0:T(8,128)(4,1)} %get-tuple-element.120) | copy-start | bytes 196612
  121.3 21.4 %copy-start.23 = (pred[256,256]{1,0:T(8,128)(4,1)S(1)}, pred[256,256]{1,0:T(8,128)(4,1)}, u32[]{:S(2)}) copy-start(pred[256,256]{1,0:T(8,128)(4,1)} %get-tuple-element.121) | copy-start | bytes 196612
  121.3 21.4 %copy-start.24 = (pred[256,256]{1,0:T(8,128)(4,1)S(1)}, pred[256,256]{1,0:T(8,128)(4,1)}, u32[]{:S(2)}) copy-start(pred[256,256]{1,0:T(8,128)(4,1)} %get-tuple-element.122) | copy-start | bytes 196612
  121.3 21.4 %copy-start.25 = (pred[256,256]{1,0:T(8,128)(4,1)S(1)}, pred[256,256]{1,0:T(8,128)(4,1)}, u32[]{:S(2)}) copy-start(pred[256,256]{1,0:T(8,128)(4,1)} %get-tuple-element.123) | copy-start | bytes 196612
  121.3 21.4 %copy-start.26 = (pred[256,256]{1,0:T(8,128)(4,1)S(1)}, pred[256,256]{1,0:T(8,128)(4,1)}, u32[]{:S(2)}) copy-start(pred[256,256]{1,0:T(8,128)(4,1)} %get-tuple-element.124) | copy-start | bytes 196612
  121.3 21.4 %copy-start.27 = (pred[256,256]{1,0:T(8,128)(4,1)S(1)}, pred[256,256]{1,0:T(8,128)(4,1)}, u32[]{:S(2)}) copy-start(pred[256,256]{1,0:T(8,128)(4,1)} %get-tuple-element.125) | copy-start | bytes 196612
  121.4 21.4 %copy-start.28 = (pred[256,256]{1,0:T(8,128)(4,1)S(1)}, pred[256,256]{1,0:T(8,128)(4,1)}, u32[]{:S(2)}) copy-start(pred[256,256]{1,0:T(8,128)(4,1)} %get-tuple-element.126) | copy-start | bytes 196612
  121.4 21.4 %copy-start.29 = (pred[256,256]{1,0:T(8,128)(4,1)S(1)}, pred[256,256]{1,0:T(8,128)(4,1)}, u32[]{:S(2)}) copy-start(pred[256,256]{1,0:T(8,128)(4,1)} %get-tuple-element.127) | copy-start | bytes 196612
  121.4 21.4 %copy-start.30 = (pred[256,256]{1,0:T(8,128)(4,1)S(1)}, pred[256,256]{1,0:T(8,128)(4,1)}, u32[]{:S(2)}) copy-start(pred[256,256]{1,0:T(8,128)(4,1)} %get-tuple-element.128) | copy-start | bytes 196612
  121.4 21.4 %copy-start.31 = (pred[256,256]{1,0:T(8,128)(4,1)S(1)}, pred[256,256]{1,0:T(8,128)(4,1)}, u32[]{:S(2)}) copy-start(pred[256,256]{1,0:T(8,128)(4,1)} %get-tuple-element.129) | copy-start | bytes 196612
  121.4 21.4 %copy-start.32 = (pred[256,256]{1,0:T(8,128)(4,1)S(1)}, pred[256,256]{1,0:T(8,128)(4,1)}, u32[]{:S(2)}) copy-start(pred[256,256]{1,0:T(8,128)(4,1)} %get-tuple-element.130) | copy-start | bytes 196612
  121.4 21.4 %copy-start.33 = (pred[256,256]{1,0:T(8,128)(4,1)S(1)}, pred[256,256]{1,0:T(8,128)(4,1)}, u32[]{:S(2)}) copy-start(pred[256,256]{1,0:T(8,128)(4,1)} %get-tuple-element.131) | copy-start | bytes 196612
  121.4 21.4 %copy-start.34 = (pred[256,256]{1,0:T(8,128)(4,1)S(1)}, pred[256,256]{1,0:T(8,128)(4,1)}, u32[]{:S(2)}) copy-start(pred[256,256]{1,0:T(8,128)(4,1)} %get-tuple-element.132) | copy-start | bytes 196612
  459.5 3.3 copy-start.2
  462.7 3.7 copy-start.1
Sparse Core Ops, SparseCore 0:
  32.9 23.6 all-gather.10
  58.1 25.4 all-gather.8
  109.6 13.7 all-gather.14
  124.7 25.4 all-gather.12

commit v3 on v2

--- a/solution.py
+++ b/solution.py
@@ -1,5 +1,3 @@
-import functools
-
 import jax
 import jax.numpy as jnp
 from jax import lax
@@ -12,7 +10,6 @@
 EPSILON = 1e-6
 F32 = jnp.float32
 BF16 = jnp.bfloat16
-TP_SWAP = ((0, 1), (1, 0))
 VMEM_LIMIT = 60 * 1024 * 1024
 
 
@@ -30,111 +27,22 @@
     return lax.dot_general(a, b, (((1,), (1,)), ((), ())), preferred_element_type=F32)
 
 
-def fixed(shape, index):
-    return pl.BlockSpec(shape, lambda *_: index, pipeline_mode=pl.Buffered(1))
-
-
-def bias_map(table, seq_len):
-    pos = jnp.arange(seq_len, dtype=jnp.int32)
-    rel = pos[:, None] - pos[None, :]
-    bucket = jnp.minimum(jnp.maximum(rel, 0), EXACT_BUCKETS)
+def bias_rows(table, seq_len):
+    at = jnp.arange(2 * seq_len, dtype=jnp.int32)
+    rel = jnp.where(at == 0, 0, 2 * seq_len - at)
+    bucket = jnp.minimum(rel, EXACT_BUCKETS)
     for threshold in THRESHOLDS:
         bucket = bucket + (rel >= threshold).astype(jnp.int32)
-    out = jnp.broadcast_to(table[:, 0][:, None, None], (table.shape[0], seq_len, seq_len))
-    for k in range(1, table.shape[1]):
-        out = jnp.where(bucket[None] == k, table[:, k][:, None, None], out)
-    return jnp.where(rel[None] >= 0, out, -jnp.inf)
+    out = jnp.broadcast_to(table[..., 0:1], table.shape[:-1] + (2 * seq_len,))
+    for k in range(1, table.shape[-1]):
+        out = jnp.where(bucket == k, table[..., k:k + 1], out)
+    return jnp.where(rel < seq_len, out, -jnp.inf)
 
 
 def softmax_bf16(scores):
     top = jnp.max(scores, axis=-1, keepdims=True)
     grown = jnp.exp(scores - top)
-    return (grown / jnp.sum(grown, axis=-1, keepdims=True)).astype(BF16)
-
-
-def attention_body(x_ref, ln_ref, wq_ref, wk_ref, wv_ref, w_other_ref, wo_ref, wo_other_ref, bias_ref, out_ref, ctx_ref):
-    x = x_ref[0]
-    seq_len = x.shape[0]
-    half = seq_len // 2
-    a = rms_rows(x, ln_ref[0])
-    inner = wq_ref.shape[2]
-    lanes = lax.broadcasted_iota(jnp.int32, (1, 128), 1)
-    first = lanes < 64
-    for side in range(2):
-        if side == 0:
-            q, k, v = (mm(a, ref[0]).astype(BF16) for ref in (wq_ref, wk_ref, wv_ref))
-        else:
-            q, k, v = (mm(a, w_other_ref[:, i * inner:(i + 1) * inner]).astype(BF16) for i in range(3))
-        for pair in range(inner // 128):
-            cols = slice(pair * 128, (pair + 1) * 128)
-            qp, kp, vp = q[:, cols], k[:, cols], v[:, cols]
-            low, high = [], []
-            for sub in range(2):
-                head = side * (inner // 64) + pair * 2 + sub
-                keep = first if sub == 0 else jnp.logical_not(first)
-                qh = jnp.where(keep, qp, jnp.zeros_like(qp))
-                s_low = mm_t(qh[:half], kp[:half]) * 0.125 + bias_ref[head, :half, :half]
-                s_high = mm_t(qh[half:], kp) * 0.125 + bias_ref[head, half:, :]
-                low.append(mm(softmax_bf16(s_low), vp[:half]))
-                high.append(mm(softmax_bf16(s_high), vp))
-            at = side * inner + pair * 128
-            ctx_ref[:half, at:at + 128] = jnp.where(first, low[0], low[1]).astype(BF16)
-            ctx_ref[half:, at:at + 128] = jnp.where(first, high[0], high[1]).astype(BF16)
-    total = mm(ctx_ref[:, :inner], wo_ref[0]) + mm(ctx_ref[:, inner:], wo_other_ref[...])
-    out_ref[0] = (x.astype(F32) + total).astype(BF16)
-
-
-def attention_layer(layer, x, ln, w_query, w_key, w_value, w_other, w_out, wo_other, bias):
-    seqs, seq_len, d_model = x.shape
-    inner = w_query.shape[2]
-    own = fixed((1, d_model, inner), (layer, 0, 0))
-    flops = 2 * seqs * seq_len * d_model * (4 * 2 * inner) + 4 * seqs * seq_len * seq_len * 2 * inner
-    return pl.pallas_call(
-        attention_body,
-        grid=(seqs,),
-        in_specs=[
-            pl.BlockSpec((1, seq_len, d_model), lambda s: (s, 0, 0)),
-            fixed((1, d_model), (0, 0)),
-            own, own, own,
-            fixed(w_other.shape, (0, 0)),
-            fixed((1, inner, d_model), (layer, 0, 0)),
-            fixed(wo_other.shape, (0, 0)),
-            fixed(bias.shape, (0, 0, 0)),
-        ],
-        out_specs=pl.BlockSpec((1, seq_len, d_model), lambda s: (s, 0, 0)),
-        out_shape=jax.ShapeDtypeStruct(x.shape, BF16),
-        scratch_shapes=[pltpu.VMEM((seq_len, 2 * inner), BF16)],
-        compiler_params=pltpu.CompilerParams(vmem_limit_bytes=VMEM_LIMIT),
-        cost_estimate=pl.CostEstimate(flops=flops, bytes_accessed=18 << 20, transcendentals=0),
-        name=f"attention{layer}",
-    )(x, ln, w_query, w_key, w_value, w_other, w_out, wo_other, bias)
-
-
-def ffn_body(h_ref, ln_ref, wg_ref, wu_ref, wd_ref, gu_other_ref, wd_other_ref, out_ref):
-    h = h_ref[...]
-    b = rms_rows(h, ln_ref[0])
-    width = wg_ref.shape[1]
-    own = (jax.nn.gelu(mm(b, wg_ref[...])) * mm(b, wu_ref[...])).astype(BF16)
-    other = (jax.nn.gelu(mm(b, gu_other_ref[:, :width])) * mm(b, gu_other_ref[:, width:])).astype(BF16)
-    total = mm(own, wd_ref[...]) + mm(other, wd_other_ref[...])
-    out_ref[...] = (h.astype(F32) + total).astype(BF16)
-
-
-def ffn_layer(rows, ln, w_gate, w_up, w_down, gu_other, wd_other, block=256):
-    n, d_model = rows.shape
-    flops = 2 * n * d_model * 6 * w_gate.shape[1]
-    row_spec = pl.BlockSpec((block, d_model), lambda i: (i, 0))
-    weights = [w_gate, w_up, w_down, gu_other, wd_other]
-    return pl.pallas_call(
-        ffn_body,
-        grid=(n // block,),
-        in_specs=[row_spec, fixed((1, d_model), (0, 0))] + [fixed(w.shape, (0, 0)) for w in weights],
-        out_specs=row_spec,
-        out_shape=jax.ShapeDtypeStruct(rows.shape, BF16),
-        compiler_params=pltpu.CompilerParams(vmem_limit_bytes=VMEM_LIMIT),
-        cost_estimate=pl.CostEstimate(flops=flops, bytes_accessed=7 << 20, transcendentals=0),
-        name="ffn",
-    )(rows, ln, *weights)
+    return (grown * (1.0 / jnp.sum(grown, axis=-1, keepdims=True))).astype(BF16)
 
 
 def axis_neighbours(tp, ep):
@@ -147,6 +55,259 @@
     return pltpu.make_async_remote_copy(
         src_ref=src, dst_ref=dst, send_sem=send, recv_sem=recv,
         device_id=(lax.axis_index('dp'), tp, ep), device_id_type=pl.DeviceIdType.MESH)
+
+
+def layers_body(hid_ref, ln_attn_ref, ln_ffn_ref, wq_hbm, wk_hbm, wv_hbm, wo_hbm, u_ref, wg_hbm, wu_hbm, wd_hbm,
+                h1_ref, h2_ref, x0_ref, x0t_ref,
+                x, a_ref, acc, w, wo, gu, wd, u_other, bias_low, bias_high, qkv, ctx, stage,
+                in_sem, own_sem, out_sem, misc_send, misc_recv, y_send, y_recv, x_send, x_recv, c_send, c_recv, d_send, d_recv):
+    tp, ep = lax.axis_index('tp'), lax.axis_index('ep')
+    other = 1 - tp
+    ep1, ep2, ep3 = axis_neighbours(tp, ep)
+    seqs, seq_len, d_model = x.shape
+    half = seq_len // 2
+    tokens = seqs * seq_len
+    quad = qkv.shape[2]
+
+    def part(count, quarter):
+        return pl.ds(pl.multiple_of(quarter * count, count), count)
+
+    my_pos = part(half, tp)
+    mine = hid_ref.at[pl.ds(tp * seqs, seqs)]
+    theirs = hid_ref.at[pl.ds(other * seqs, seqs)]
+
+    sources, places = [], []
+    for layer in range(2):
+        for kind, hbm in enumerate((wq_hbm, wk_hbm, wv_hbm)):
+            sources.append(hbm.at[layer, :, part(128, ep)])
+            places.append(lambda q, layer=layer, kind=kind: w.at[layer, 1, kind, :, part(128, q)])
+        sources.append(wo_hbm.at[layer, part(128, ep), :])
+        places.append(lambda q, layer=layer: wo.at[layer, 1, part(128, q), :])
+        if layer == 0:
+            for kind, hbm in enumerate((wg_hbm, wu_hbm)):
+                sources.append(hbm.at[part(256, ep), :])
+                places.append(lambda q, kind=kind: gu.at[1, kind, part(256, q), :])
+            sources.append(wd_hbm.at[part(64, ep), :])
+            places.append(lambda q: wd.at[1, part(64, q), :])
+
+    own_x = pltpu.make_async_copy(mine, x.at[:, my_pos, :], in_sem.at[0])
+    own_stage = pltpu.make_async_copy(theirs, stage, in_sem.at[1])
+    own_x.start()
+    own_loads = []
+    for layer in range(2):
+        for kind, hbm in enumerate((wq_hbm, wk_hbm, wv_hbm)):
+            own_loads.append((hbm.at[layer], w.at[layer, 0, kind]))
+        own_loads.append((wo_hbm.at[layer], wo.at[layer, 0]))
+        if layer == 0:
+            own_loads += [(wg_hbm, gu.at[0, 0]), (wu_hbm, gu.at[0, 1]), (wd_hbm, wd.at[0])]
+    own_loads = [pltpu.make_async_copy(s, d, own_sem.at[n]) for n, (s, d) in enumerate(own_loads)]
+    for load in own_loads:
+        load.start()
+    own_stage.start()
+
+    barrier = pltpu.get_barrier_semaphore()
+    for peer_tp, peer_ep in ((other, ep), (tp, ep2), (tp, ep1)):
+        pl.semaphore_signal(barrier, inc=1, device_id=(lax.axis_index('dp'), peer_tp, peer_ep), device_id_type=pl.DeviceIdType.MESH)
+    pl.semaphore_wait(barrier, 3)
+
+    def arrived(ref, sem):
+        remote(ref, ref, misc_send.at[0], sem, tp, ep).wait_recv()
+
+    pieces = range(len(sources))
+    send_entry = remote(theirs, x.at[:, my_pos, :], misc_send.at[0], misc_recv.at[0], other, ep)
+    send_u = remote(u_ref, u_other, misc_send.at[1], misc_recv.at[1], other, ep)
+    send_rest = remote(mine, x0t_ref.at[:, my_pos, :], misc_send.at[2], misc_recv.at[2], other, ep)
+    y_copies = [remote(sources[n], places[n](ep), y_send.at[n], y_recv.at[n], other, ep) for n in pieces]
+    x_copies = [remote(places[n](ep), places[n](ep), x_send.at[n], x_recv.at[n], tp, ep2) for n in pieces]
+    c_copies = [remote(places[n](ep), places[n](ep), c_send.at[n], c_recv.at[n], tp, ep1) for n in pieces]
+    d_copies = [remote(places[n](ep2), places[n](ep2), d_send.at[n], d_recv.at[n], tp, ep1) for n in pieces]
+    send_u.start()
+    send_entry.start()
+    for copy in y_copies:
+        copy.start()
+    send_rest.start()
+
+    def pass_on(n):
+        arrived(places[n](ep), y_recv.at[n])
+        x_copies[n].start()
+        c_copies[n].start()
+
+    def pass_across(n):
+        arrived(places[n](ep2), x_recv.at[n])
+        d_copies[n].start()
+
+    def complete(n):
+        arrived(places[n](ep1), c_recv.at[n])
+        arrived(places[n](ep3), d_recv.at[n])
+
+    def build_bias(rows_ref, side):
+        @pl.loop(0, 8)
+        def _(n):
+            layer, pair = n // 4, lax.rem(n, 4)
+            for sub in range(2):
+                row = rows_ref[layer, pair * 2 + sub]
+                wide = pltpu.roll(jnp.broadcast_to(row, (seq_len, 2 * seq_len)), 0, 1, stride=1, stride_axis=0)
+                at = slice(sub * half, (sub + 1) * half)
+                place = layer * 8 + side * 4 + pair
+                bias_low[place, at, :] = wide[:half, :half]
+                bias_high[place, at, :] = wide[half:, :seq_len]
+
+    def begin_layer(layer):
+        @pl.loop(0, seqs)
+        def _(s):
+            rows = part(seq_len, s)
+            a_ref[rows, :] = rms_rows(x[s], ln_attn_ref[layer])
+            acc[rows, :] = x[s].astype(F32)
+
+    def end_layer():
+        @pl.loop(0, seqs)
+        def _(s):
+            x[s] = acc[part(seq_len, s), :].astype(BF16)
+
+    first = lax.broadcasted_iota(jnp.int32, (1, 128), 1) < 64
+
+    def heads(layer, side, block):
+        cols = slice(block * quad, (block + 1) * quad)
+        for kind in range(3):
+            qkv[kind] = mm(a_ref[...], w[layer, side, kind, :, cols]).astype(BF16)
+
+        @pl.loop(0, seqs)
+        def _(s):
+            rows = part(seq_len, s)
+            for pair in range(quad // 128):
+                lanes = slice(pair * 128, (pair + 1) * 128)
+                place = layer * 8 + side * 4 + block * (quad // 128) + pair
+                q, k, v = (qkv[kind, rows, lanes] for kind in range(3))
+                none = jnp.zeros_like(q[:half])
+                outs = []
+                for upper in range(2):
+                    qs = q[half:] if upper else q[:half]
+                    ks, vs = (k, v) if upper else (k[:half], v[:half])
+                    both = jnp.concatenate([jnp.where(first, qs, none), jnp.where(first, none, qs)], axis=0)
+                    bias = bias_high[place] if upper else bias_low[place]
+                    got = mm(softmax_bf16(mm_t(both, ks) * 0.125 + bias), vs)
+                    outs.append(jnp.where(first, got[:half], got[half:]))
+                ctx[rows, lanes] = jnp.concatenate(outs, axis=0).astype(BF16)
+
+        @pl.loop(0, seqs)
+        def _(s):
+            rows = part(seq_len, s)
+            acc[rows, :] += mm(ctx[rows, :], wo[layer, side, cols, :])
+
+    def dense(s):
+        h = x[s]
+        b = rms_rows(h, ln_ffn_ref[0])
+        total = h.astype(F32)
+        for side in range(2):
+            hid = (jax.nn.gelu(mm(b, gu[side, 0])) * mm(b, gu[side, 1])).astype(BF16)
+            total = total + mm(hid, wd[side])
+        x[s] = total.astype(BF16)
+
+    build_bias(u_ref, 0)
+    arrived(u_other, misc_recv.at[1])
+    build_bias(u_other, 1)
+    own_stage.wait()
+    own_x0t = pltpu.make_async_copy(stage, x0t_ref.at[:, my_pos, :], out_sem.at[0])
+    own_x0t.start()
+
+    own_x.wait()
+    arrived(x.at[:, part(half, other), :], misc_recv.at[0])
+    out_x0 = pltpu.make_async_copy(x, x0_ref, out_sem.at[1])
+    out_x0.start()
+    begin_layer(0)
+    for n in range(4):
+        own_loads[n].wait()
+    heads(0, 0, 0)
+    heads(0, 0, 1)
+    for n in range(4):
+        pass_on(n)
+    for n in range(4):
+        pass_across(n)
+    for n in range(4, 7):
+        pass_on(n)
+    for n in range(4):
+        complete(n)
+    heads(0, 1, 0)
+    pass_on(7)
+    heads(0, 1, 1)
+    for n in range(4, 7):
+        pass_across(n)
+    out_x0.wait()
+    end_layer()
+    for n in range(4, 7):
+        own_loads[n].wait()
+        complete(n)
+    pass_on(8)
+
+    @pl.loop(0, seqs // 2)
+    def _(s):
+        dense(s)
+
+    pass_on(9)
+
+    @pl.loop(seqs // 2, seqs)
+    def _(s):
+        dense(s)
+
+    out_h1 = pltpu.make_async_copy(x, h1_ref, out_sem.at[2])
+    out_h1.start()
+    begin_layer(1)
+    for n in range(7, 11):
+        own_loads[n].wait()
+    heads(1, 0, 0)
+    pass_on(10)
+    heads(1, 0, 1)
+    for n in range(7, 11):
+        pass_across(n)
+    for n in range(7, 11):
+        complete(n)
+    heads(1, 1, 0)
+    heads(1, 1, 1)
+    out_h1.wait()
+    end_layer()
+    out_h2 = pltpu.make_async_copy(x, h2_ref, out_sem.at[3])
+    out_h2.start()
+
+    arrived(x0t_ref.at[:, part(half, other), :], misc_recv.at[2])
+    own_x0t.wait()
+    for copy in [send_entry, send_u, send_rest] + y_copies + x_copies + c_copies + d_copies:
+        copy.wait_send()
+    out_h2.wait()
+
+
+def dense_layers(hidden_in, ln_attn, ln_ffn, w_query, w_key, w_value, w_out, bias_u, w_gate, w_up, w_down):
+    batch, positions, d_model = hidden_in.shape
+    seqs, seq_len = batch // 2, 2 * positions
+    inner = w_query.shape[2]
+    any_spec = pl.BlockSpec(memory_space=pl.ANY)
+    vmem_spec = pl.BlockSpec(memory_space=pltpu.VMEM)
+    dma = pltpu.SemaphoreType.DMA
+    shape = jax.ShapeDtypeStruct((seqs, seq_len, d_model), BF16)
+    return pl.pallas_call(
+        layers_body,
+        in_specs=[any_spec, vmem_spec, vmem_spec] + [any_spec] * 4 + [vmem_spec] + [any_spec] * 3,
+        out_specs=[any_spec] * 4,
+        out_shape=[shape] * 4,
+        scratch_shapes=[
+            pltpu.VMEM(shape.shape, BF16),
+            pltpu.VMEM((seqs * seq_len, d_model), BF16),
+            pltpu.VMEM((seqs * seq_len, d_model), F32),
+            pltpu.VMEM((2, 2, 3, d_model, inner), BF16),
+            pltpu.VMEM((2, 2, inner, d_model), BF16),
+            pltpu.VMEM((2, 2) + w_gate.shape, BF16),
+            pltpu.VMEM((2,) + w_down.shape, BF16),
+            pltpu.VMEM(bias_u.shape, F32),
+            pltpu.VMEM((16, seq_len, seq_len // 2), F32),
+            pltpu.VMEM((16, seq_len, seq_len), F32),
+            pltpu.VMEM((3, seqs * seq_len, 256), BF16),
+            pltpu.VMEM((seqs * seq_len, 256), BF16),
+            pltpu.VMEM((seqs, positions, d_model), BF16),
+            dma((2,)), dma((11,)), dma((4,)), dma((3,)), dma((3,)),
+        ] + [dma((11,))] * 8,
+        compiler_params=pltpu.CompilerParams(vmem_limit_bytes=VMEM_LIMIT, collective_id=1, has_side_effects=True),
+        cost_estimate=pl.CostEstimate(flops=32_000_000_000, bytes_accessed=40 << 20, transcendentals=0),
+        name="dense_layers",
+    )(hidden_in, ln_attn, ln_ffn, w_query, w_key, w_value, w_out, bias_u, w_gate, w_up, w_down)
 
 
 def moe_body(h2_ref, h1_ref, x0_ref, x0t_ref, slot_row_ref, slot_col_ref, ids_ref, ln_ref, ln_attn_ref, router_ref,
@@ -404,57 +565,18 @@
     cache_spec = P(None, ('dp', 'ep'), 'tp', None, None)
     in_specs = (act_spec, P(), P(), col_spec, col_spec, col_spec, row_spec, row_spec,
                 P(None, 'tp'), P(None, 'tp'), P('tp', None), P(), expert_spec, expert_spec, act_spec)
-    tp_n, ep_n = mesh.shape['tp'], mesh.shape['ep']
 
     def device_fn(hidden_in, ln_attn, ln_ffn, w_query, w_key, w_value, w_out, bias_table, w_gate, w_up, w_down, w_router, expert_in, expert_out, expert_ids):
         batch, positions, d_model = hidden_in.shape
-        half = batch // 2
-        tp, ep = lax.axis_index('tp'), lax.axis_index('ep')
-        swap = lambda value: lax.ppermute(value, 'tp', TP_SWAP)
-        spread = lambda value: lax.all_gather(value, 'ep', axis=0, tiled=False)
-
-        def quarter(weight):
-            rows = weight.shape[0] // ep_n
-            return lax.dynamic_slice_in_dim(weight, ep * rows, rows, 0)
-
-        def whole_seq(own, other):
-            return jnp.where(tp == 0, jnp.concatenate([own, other], axis=1), jnp.concatenate([other, own], axis=1))
-
-        def qkv_other(layer):
-            part = jnp.concatenate([quarter(w[layer]) for w in (w_query, w_key, w_value)], axis=1)
-            return spread(swap(part)).reshape(d_model, -1)
-
-        kept = lax.dynamic_slice_in_dim(hidden_in, tp * half, half, 0)
-        given = lax.dynamic_slice_in_dim(hidden_in, (1 - tp) * half, half, 0)
-
-        wqkv0 = qkv_other(0)
-        x0 = whole_seq(kept, swap(given))
-        out_part0 = quarter(w_out[0])
-        down_part = quarter(w_down)
-        gu_part = jnp.concatenate([quarter(w_gate), quarter(w_up)], axis=1)
-        tail0 = jnp.concatenate([out_part0, down_part, gu_part.reshape(-1, d_model)], axis=0)
-        tail0 = spread(swap(tail0))
-        n_out, n_down = out_part0.shape[0], down_part.shape[0]
-        wo0 = tail0[:, :n_out].reshape(-1, d_model)
-        wd_other = tail0[:, n_out:n_out + n_down].reshape(-1, d_model)
-        gu_other = tail0[:, n_out + n_down:].reshape(d_model, -1)
-        wqkv1 = qkv_other(1)
-        wo1 = spread(swap(quarter(w_out[1]))).reshape(-1, d_model)
-        bias_all = jnp.concatenate([bias_table, swap(bias_table)], axis=1)
-
         num_experts = w_router.shape[1]
         tokens = batch * positions
         capacity = 4 * tokens // num_experts
         choices = expert_ids.reshape(tokens, 2)
         slots = slot_table(choices, num_experts, capacity)
-
-        h = attention_layer(0, x0, ln_attn[0:1], w_query, w_key, w_value, wqkv0, w_out, wo0, bias_map(bias_all[0], tp_n * positions))
-        h1 = ffn_layer(h.reshape(tokens, d_model), ln_ffn[0:1], w_gate, w_up, w_down, gu_other, wd_other).reshape(h.shape)
-        h2 = attention_layer(1, h1, ln_attn[1:2], w_query, w_key, w_value, wqkv1, w_out, wo1, bias_map(bias_all[1], tp_n * positions))
-
-        x0_theirs = whole_seq(given, swap(kept))
+        bias_u = bias_rows(bias_table, 2 * positions)[:, :, None, :]
+        h1, h2, x0, x0t = dense_layers(hidden_in, ln_attn, ln_ffn, w_query, w_key, w_value, w_out, bias_u, w_gate, w_up, w_down)
         hidden, k_cache, v_cache, _ = moe_layer(
-            h2, h1, x0, x0_theirs, slots, choices, ln_ffn[1:2], ln_attn, w_router, expert_in, expert_out, w_key, w_value)
+            h2, h1, x0, x0t, slots, choices, ln_ffn[1:2], ln_attn, w_router, expert_in, expert_out, w_key, w_value)
         return hidden.reshape(hidden_in.shape), jnp.swapaxes(k_cache, 3, 4), jnp.swapaxes(v_cache, 3, 4)
 
     return jax.shard_map(device_fn, mesh=mesh, in_specs=in_specs, out_specs=(act_spec, cache_spec, cache_spec), check_vma=False)

time: 482 us -> 351 us (0.73)
  other arithmetic: 63.4 us -> 2.95 us
  waiting for transfers between devices: 58.1 us -> 0 us
  Pallas kernels: 284 us -> 326 us
  local copies, waits for them, and re-layouts: 43.7 us -> 16.7 us
  between operations: 14.9 us -> 1.06 us
  starting transfers between devices: 11.1 us -> 0 us
    ppermute x7 -> x0, waiting for transfers between devices: 58.1 us -> none  [device_fn(): swap = lambda value: lax.ppermute(value, 'tp', TP_SWAP)]
    select_n x4 -> x1, other arithmetic: 47.4 us -> 2.04 us  [bias_rows(): return jnp.where(rel < seq_len, out, -jnp.inf)]
    pallas_call x3 -> x1, Pallas kernels: 80.9 us -> 123 us  [dense_layers(): pl.pallas_call(layers_body, in_specs=[any_spec, vmem_spec, vmem_spec] + [...]
    eq x15, other arithmetic: 12.2 us -> 0.36 us  [bias_rows(): out = jnp.where(bucket == k, table[..., k:k + 1], out)]
    slice x11 -> x2, local copies, waits for them, and re-layouts: 14.5 us -> 2.95 us  [bias_rows(): out = jnp.where(bucket == k, table[..., k:k + 1], out)]
    ppermute x7 -> x0, starting transfers between devices: 10.7 us -> none  [device_fn(): swap = lambda value: lax.ppermute(value, 'tp', TP_SWAP)]
    dynamic_slice x9 -> x0, local copies, waits for them, and re-layouts: 6.95 us -> none  [the longest x8 5.14 us: quarter(): return lax.dynamic_slice_in_dim(weight, ep * rows, rows, 0)]
    unnamed x80 -> x15, local copies, waits for them, and re-layouts: 15.2 us -> 10.9 us
  transfers between devices with their start and end apart: 11 -> 0, of which waited for: 3 -> 0; matrix products, arithmetic and copies ran while one was open for 19% -> 0% of each run, Pallas kernels for 9% -> 0%
where the time goes in v3:
time: 351 us; the launch traced here: 347 us
  Pallas kernels  326 us (93%)
  local copies, waits for them, and re-layouts  16.7 us (5%)
    pallas_call x1, Pallas kernels, moe_layer(): pl.pallas_call(moe_body, in_specs=[any_spec] * 4 + [vmem_spec] * 6 + [any...  203 us
    pallas_call x1, Pallas kernels, dense_layers(): pl.pallas_call(layers_body, in_specs=[any_spec, vmem_spec, vmem_spec] + [...  123 us
    unnamed x15, local copies, waits for them, and re-layouts  10.9 us

profile of v3, /device:TPU:0, one launch (start us, length us, event | category | flops | bytes accessed | tf_op | source)
XLA Modules:
  0.0 347.3 jit_solution(4861254830415102730)
XLA Ops:
  0.6 0.1 eq.321
  1.1 1.3 slice.151.ln_ref
  2.4 1.4 slice_reduce_fusion.30
  3.8 1.6 slice_reduce_fusion.31
  5.4 2.0 broadcast_select_fusion.31.u_ref
  7.4 0.9 copy.28
  8.3 0.0 copy-start
  8.3 0.2 copy.29
  8.5 0.1 bitcast_compare_fusion
  8.7 0.6 fusion
  9.2 0.0 copy-start.4
  9.3 0.2 fusion.3
  9.4 0.1 fusion.2
  9.6 0.3 copy.32
  9.9 0.2 copy.31
  10.1 0.1 add_select_fusion.slot_col_ref
  10.2 0.0 copy-done
  10.2 0.0 copy-start.3
  10.2 0.8 copy.33.slot_row_ref
  11.0 0.0 copy-done.4
  11.0 1.0 copy.34.router_ref
  12.0 123.1 %dense_layers.1 = (bf16[4,256,1024]{2,1,0:T(8,128)(2,1)}, bf16[4,256,1024]{2,1,0:T(8,128)(2,1)}, bf16[4,256,1024]{2,1,0:T(8,128)(2,1)}, bf16[4,256,1024]{2,1,0:T(8,128)(2,1)}) custom-call(bf16[8,128,1024]{2,1,0:T(8,128)(2,1)} %hid_ref.1, f32[2,1024]{1,0:T(2,128)} %ln_attn_ref.3, f32[2,1024]{1,0:T(2,128)} %ln_ffn_ref.1, bf16[2,1024,512]{2,1,0:T(8,128)(2,1)} %wq_hbm.1, ...), custom_call_target="tpu_custom_call" | custom-call | flops 32000000000 | bytes 41943040 | tf_op jit(solution)/shard_map/dense_layers/pallas_call | solution.py:286
  135.2 0.0 copy-done.3
  135.2 202.9 %moe.1 = (bf16[1024,1024]{1,0:T(8,128)(2,1)}, bf16[2,8,8,64,256]{4,3,2,1,0:T(8,128)(2,1)}, bf16[2,8,8,64,256]{4,3,2,1,0:T(8,128)(2,1)}, bf16[4,256,1024]{2,1,0:T(8,128)(2,1)}) custom-call(bf16[4,256,1024]{2,1,0:T(8,128)(2,1)} %get-tuple-element.10.h2_ref, bf16[4,256,1024]{2,1,0:T(8,128)(2,1)} %get-tuple-element.11.h1_ref, ...), custom_call_target="tpu_custom_call" | custom-call | flops 40000000000 | bytes 67108864 | tf_op jit(solution)/shard_map/moe/pallas_call | solution.py:518
  338.1 0.0 copy-start.2
  338.1 3.2 copy.40
  341.4 0.0 copy-done.2
  341.4 0.0 copy-start.1
  341.4 2.1 copy.41
  343.5 1.6 copy-done.1
  345.1 2.0 copy.42
  (19 shorter events, 0.4 us)
Async XLA Ops:
  8.3 1.9 copy-start
  9.2 1.8 copy-start.4
  10.2 124.9 %copy-start.3 = (s32[1024,2]{1,0:T(8,128)}, s32[1024,2]{1,0:T(8,128)S(1)}, u32[]{:S(2)}) copy-start(s32[1024,2]{1,0:T(8,128)S(1)} %add_select_fusion.slot_col_ref) | copy-start | bytes 24580
  338.1 3.3 copy-start.2
  341.4 3.7 %copy-start.1 = (bf16[2,8,8,64,256]{4,3,2,1,0:T(8,128)(2,1)S(1)}, bf16[2,8,8,64,256]{4,3,2,1,0:T(8,128)(2,1)}, u32[]{:S(2)}) copy-start(bf16[2,8,8,64,256]{4,3,2,1,0:T(8,128)(2,1)} %get-tuple-element.16) | copy-start | bytes 12582916
